TPU v7x, 8 devices: a whole 2x2x1 slice. The times are simulated.
8 devices in a mesh: dp: 2 (over z, y), tp: 4 (over x, core).
Axes of the slice: x: 2, y: 2, z: 1, core: 2. Of those that a mesh axis runs over, the one named last changes fastest.
Arguments:
- x_in: bfloat16 [8, 1024, 640], P('dp', 'tp'), parts along dimension 0
- grad_y: bfloat16 [8, 1024, 640], P('dp', 'tp'), parts along dimension 0
- pad_mask: int32 [8, 1024], P('dp'), parts along dimension 0
- ln1_gain: float32 [640], replicated
- ln1_bias: float32 [640], replicated
- w_qkv: bfloat16 [3, 640, 20, 32], P(None, None, 'tp')
- b_qkv: float32 [3, 20, 32], P(None, 'tp')
- w_out: bfloat16 [20, 32, 640], P('tp')
- b_out: float32 [640], replicated
- ln2_gain: float32 [640], replicated
- ln2_bias: float32 [640], replicated
- w_up: bfloat16 [640, 2560], P(None, 'tp')
- b_up: float32 [2560], P('tp')
- w_down: bfloat16 [2560, 640], P('tp')
- b_down: float32 [640], replicated
Outputs:
- output 1: bfloat16 [8, 1024, 640], P('dp', 'tp'), parts along dimension 0
- output 2: bfloat16 [8, 1024, 640], P('dp', 'tp'), parts along dimension 0
- output 3: float32 [1280], P('dp'), parts along dimension 0
- output 4: float32 [1280], P('dp'), parts along dimension 0
- output 5: float32 [6, 640, 20, 32], P('dp', None, 'tp'), parts along dimension 0
- output 6: float32 [6, 20, 32], P('dp', 'tp'), parts along dimension 0
- output 7: float32 [40, 32, 640], P(('dp', 'tp')), parts along dimension 0
- output 8: float32 [1280], P('dp'), parts along dimension 0
- output 9: float32 [1280], P('dp'), parts along dimension 0
- output 10: float32 [1280], P('dp'), parts along dimension 0
- output 11: float32 [1280, 2560], P('dp', 'tp'), parts along dimension 0
- output 12: float32 [5120], P(('dp', 'tp')), parts along dimension 0
- output 13: float32 [5120, 640], P(('dp', 'tp')), parts along dimension 0
- output 14: float32 [1280], P('dp'), parts along dimension 0
There are 2 independent parts. A program takes and returns all parts, laid end to end along the dimension named above; an argument that names none is the same for every part.
All inputs are finite; a program needn't handle non-finite values.
Results may differ from a plain program's by a relative error of at most 0.0125188.
Values are sent between devices in bfloat16 or wider.
A program may use at most 1 GiB of HBM per device.

v0:
```python
import jax
import jax.numpy as jnp
from jax import lax
from jax.sharding import PartitionSpec as P

LN_EPS = 1e-5
ROPE_BASE = 10000.0
INV_SQRT2 = 0.7071067811865476
INV_SQRT_2PI = 0.3989422804014327
NEG_LARGE = -1e30


def layer_norm(values, ln_gain, ln_bias):
    centered = values - jnp.mean(values, axis=-1, keepdims=True)
    inv_std = lax.rsqrt(jnp.mean(centered * centered, axis=-1, keepdims=True) + LN_EPS)
    x_hat = centered * inv_std
    return x_hat * ln_gain + ln_bias, x_hat, inv_std


def layer_norm_grad(d_out, x_hat, inv_std, ln_gain):
    d_hat = d_out * ln_gain
    return inv_std * (d_hat - jnp.mean(d_hat, axis=-1, keepdims=True) - x_hat * jnp.mean(d_hat * x_hat, axis=-1, keepdims=True))


def rope_tables(seq_len, head_dim):
    half_dim = head_dim // 2
    inv_freq = ROPE_BASE ** (-2.0 * jnp.arange(half_dim, dtype=jnp.float32) / head_dim)
    angles = jnp.arange(seq_len, dtype=jnp.float32)[:, None] * inv_freq[None, :]
    angles = jnp.concatenate([angles, angles], axis=-1)
    return jnp.cos(angles)[:, None, :], jnp.sin(angles)[:, None, :]


def rotate(tensor, cos_tab, sin_tab):
    half_dim = tensor.shape[-1] // 2
    swapped = jnp.concatenate([-tensor[..., half_dim:], tensor[..., :half_dim]], axis=-1)
    return tensor * cos_tab + swapped * sin_tab


def rotate_back(grad_in, cos_tab, sin_tab):
    half_dim = grad_in.shape[-1] // 2
    scaled = grad_in * sin_tab
    swapped = jnp.concatenate([scaled[..., half_dim:], -scaled[..., :half_dim]], axis=-1)
    return grad_in * cos_tab + swapped


def solution(mesh):
    act_spec = P('dp', 'tp', None)
    rep_vec = P(None)
    part_vec = P('dp')
    in_specs = (act_spec, act_spec, P('dp', None), rep_vec, rep_vec, P(None, None, 'tp', None), P(None, 'tp', None),
                P('tp', None, None), rep_vec, rep_vec, rep_vec, P(None, 'tp'), P('tp'), P('tp', None), rep_vec)
    out_specs = (act_spec, act_spec, part_vec, part_vec, P('dp', None, 'tp', None), P('dp', 'tp', None),
                 P(('dp', 'tp'), None, None), part_vec, part_vec, part_vec, P('dp', 'tp'), P(('dp', 'tp')),
                 P(('dp', 'tp'), None), part_vec)

    def device_step(x_in, grad_y, pad_mask, ln1_gain, ln1_bias, w_qkv, b_qkv, w_out, b_out, ln2_gain, ln2_bias, w_up, b_up, w_down, b_down):
        seq_len = pad_mask.shape[1]
        head_dim = w_qkv.shape[3]
        q_scale = head_dim ** -0.5
        cos_tab, sin_tab = rope_tables(seq_len, head_dim)
        key_ok = (pad_mask > 0)[:, None, None, :]
        x_f = x_in.astype(jnp.float32)
        h1_f, x_hat1, inv_std1 = layer_norm(x_f, ln1_gain, ln1_bias)
        h1_full = lax.all_gather(h1_f.astype(jnp.bfloat16), 'tp', axis=1, tiled=True)
        qkv_all = jnp.einsum('bsd,idhk->ibshk', h1_full, w_qkv, preferred_element_type=jnp.float32) + b_qkv[:, None, None]
        q_rot = rotate(qkv_all[0] * q_scale, cos_tab, sin_tab).astype(jnp.bfloat16)
        k_rot = rotate(qkv_all[1], cos_tab, sin_tab).astype(jnp.bfloat16)
        v_heads = qkv_all[2].astype(jnp.bfloat16)
        scores = jnp.einsum('bqhk,bshk->bhqs', q_rot, k_rot, preferred_element_type=jnp.float32)
        attn_probs = jax.nn.softmax(jnp.where(key_ok, scores, NEG_LARGE), axis=-1)
        probs_low = attn_probs.astype(jnp.bfloat16)
        attn_o = jnp.einsum('bhqs,bshk->bqhk', probs_low, v_heads, preferred_element_type=jnp.float32).astype(jnp.bfloat16)
        attn_part = jnp.einsum('cril,ile->cre', attn_o, w_out, preferred_element_type=jnp.float32)
        attn_sum = lax.psum_scatter(attn_part, 'tp', scatter_dimension=1, tiled=True)
        x1_f = (x_f + (attn_sum + b_out)).astype(jnp.bfloat16).astype(jnp.float32)
        h2_f, x_hat2, inv_std2 = layer_norm(x1_f, ln2_gain, ln2_bias)
        h2_full = lax.all_gather(h2_f.astype(jnp.bfloat16), 'tp', axis=1, tiled=True)
        pre_act = jnp.einsum('bsd,df->bsf', h2_full, w_up, preferred_element_type=jnp.float32) + b_up
        erf_term = lax.erf(pre_act * INV_SQRT2)
        act_b = (0.5 * pre_act * (1.0 + erf_term)).astype(jnp.bfloat16)
        gelu_slope = 0.5 * (1.0 + erf_term) + pre_act * jnp.exp(-0.5 * pre_act * pre_act) * INV_SQRT_2PI
        mlp_part = jnp.einsum('bsf,fd->bsd', act_b, w_down, preferred_element_type=jnp.float32)
        mlp_sum = lax.psum_scatter(mlp_part, 'tp', scatter_dimension=1, tiled=True)
        y_out = (x1_f + (mlp_sum + b_down)).astype(jnp.bfloat16)
        dy_full = lax.all_gather(grad_y, 'tp', axis=1, tiled=True)
        dy_f = grad_y.astype(jnp.float32)
        grad_w_down = jnp.einsum('bsf,bsd->fd', act_b, dy_full, preferred_element_type=jnp.float32)
        d_act = jnp.einsum('bsd,fd->bsf', dy_full, w_down, preferred_element_type=jnp.float32)
        d_pre = d_act * gelu_slope
        grad_b_up = jnp.sum(d_pre, axis=(0, 1))
        d_pre_b = d_pre.astype(jnp.bfloat16)
        grad_w_up = jnp.einsum('bsd,bsf->df', h2_full, d_pre_b, preferred_element_type=jnp.float32)
        d_h2_part = jnp.einsum('bsf,df->bsd', d_pre_b, w_up, preferred_element_type=jnp.float32)
        d_h2 = lax.psum_scatter(d_h2_part, 'tp', scatter_dimension=1, tiled=True)
        d_x1 = dy_f + layer_norm_grad(d_h2, x_hat2, inv_std2, ln2_gain)
        mid_sums = lax.psum(jnp.stack([jnp.sum(dy_f, axis=(0, 1)), jnp.sum(d_h2 * x_hat2, axis=(0, 1)),
                                       jnp.sum(d_h2, axis=(0, 1)), jnp.sum(d_x1, axis=(0, 1))]), 'tp')
        d_x1_full = lax.all_gather(d_x1.astype(jnp.bfloat16), 'tp', axis=1, tiled=True)
        grad_w_out = jnp.einsum('bshk,bsd->hkd', attn_o, d_x1_full, preferred_element_type=jnp.float32)
        d_attn_o = jnp.einsum('bsd,hkd->bshk', d_x1_full, w_out, preferred_element_type=jnp.float32).astype(jnp.bfloat16)
        d_value = jnp.einsum('bhqs,bqhk->bshk', probs_low, d_attn_o, preferred_element_type=jnp.float32)
        d_probs = jnp.einsum('bqhk,bshk->bhqs', d_attn_o, v_heads, preferred_element_type=jnp.float32)
        d_scores = (attn_probs * (d_probs - jnp.sum(d_probs * attn_probs, axis=-1, keepdims=True))).astype(jnp.bfloat16)
        d_query = jnp.einsum('bhqs,bshk->bqhk', d_scores, k_rot, preferred_element_type=jnp.float32)
        d_key = jnp.einsum('bhqs,bqhk->bshk', d_scores, q_rot, preferred_element_type=jnp.float32)
        d_qkv = jnp.stack([rotate_back(d_query, cos_tab, sin_tab) * q_scale, rotate_back(d_key, cos_tab, sin_tab), d_value])
        grad_b_qkv = jnp.sum(d_qkv, axis=(1, 2))
        d_qkv_b = d_qkv.astype(jnp.bfloat16)
        grad_w_qkv = jnp.einsum('bsd,ibshk->idhk', h1_full, d_qkv_b, preferred_element_type=jnp.float32)
        d_h1_part = jnp.einsum('ibshk,idhk->bsd', d_qkv_b, w_qkv, preferred_element_type=jnp.float32)
        d_h1 = lax.psum_scatter(d_h1_part, 'tp', scatter_dimension=1, tiled=True)
        ln1_sums = lax.psum(jnp.stack([jnp.sum(d_h1 * x_hat1, axis=(0, 1)), jnp.sum(d_h1, axis=(0, 1))]), 'tp')
        grad_x = (d_x1 + layer_norm_grad(d_h1, x_hat1, inv_std1, ln1_gain)).astype(jnp.bfloat16)
        return (y_out, grad_x, ln1_sums[0], ln1_sums[1], grad_w_qkv, grad_b_qkv, grad_w_out, mid_sums[3],
                mid_sums[1], mid_sums[2], grad_w_up, grad_b_up, grad_w_down, mid_sums[0])

    return jax.shard_map(device_step, mesh=mesh, in_specs=in_specs, out_specs=out_specs, check_vma=False)
```

profile of v0, /device:TPU:0, one launch (start us, length us, event | category | flops | bytes accessed | tf_op | source)
XLA Modules:
  0.0 828.2 jit_solution(6503234347765761631)
XLA Ops:
  7.3 1.7 convert_reduce_fusion.1
  9.0 1.9 fusion.54
  11.0 0.6 copy-done.26
  11.5 1.6 fusion.47
  13.2 0.0 reduce-scatter.5.cloned.1.call-start
  13.3 0.1 iota_multiply_fusion
  13.3 1.0 fusion.107
  14.3 39.4 %all-gather.5.cloned.1.call-done = bf16[4,1024,640]{2,1,0:T(8,128)(2,1)} async-done(((bf16[4,256,640]{2,1,0:T(8,128)(2,1)}), bf16[4,1024,640]{2,1,0:T(8,128)(2,1)}) %all-gather.5.cloned.1.call-update) | async-done | bytes 5242896 | tf_op jit(solution)/shard_map/all_gather | solution.py:64
  53.7 5.2 add_bitcast_fusion
  59.0 0.5 fusion.70
  59.5 0.3 slice_bitcast_fusion
  59.8 1.0 slice_negate_fusion.2
  60.9 1.8 copy-done.5
  62.7 2.4 fusion.60
  65.1 35.2 %fusion.115 = (f32[4,5,1024]{2,1,0:T(8,128)}, f32[4,5,1024,1024]{2,3,1,0:T(8,128)}) fusion(pred[4,1024]{1,0:T(4,128)(4,1)S(1)} %broadcast_compare_fusion, bf16[4,1024,5,32]{1,3,2,0:T(8,128)(2,1)S(1)} %get-tuple-element.49, bf16[4,1024,5,32]{1,3,2,0:T(8,128)(2,1)} %get-tuple-element.48), kind=kOutput, calls=%fused_computation.150 | convolution fusion | flops 1405092864 | bytes 86593536 | tf_op jit(solution)/shard_map/sub | solution.py:70
  100.4 28.1 %fusion.83 = bf16[4,1024,5,32]{1,3,2,0:T(8,128)(2,1)S(1)} fusion(f32[3,4,1024,5,32]{2,4,3,0,1:T(8,128)} %copy-done.5, f32[4,5,1024,1024]{2,3,1,0:T(8,128)} %get-tuple-element.68, f32[4,5,1024]{2,1,0:T(8,128)} %get-tuple-element.67), kind=kOutput, calls=%fused_computation.104 | convolution fusion | flops 1384775680 | bytes 86638592 | tf_op jit(solution)/shard_map/bhqs,bshk->bqhk/dot_general | solution.py:72
  128.5 7.0 convolution_bitcast_fusion
  135.5 0.4 all-gather.7.cloned.1.call-start
  135.9 77.6 %reduce-scatter.5.cloned.1.call-done = f32[4,256,640]{2,1,0:T(8,128)} async-done(((f32[4,1024,640]{2,1,0:T(8,128)}), f32[4,256,640]{2,1,0:T(8,128)}) %reduce-scatter.5.cloned.1.call-update) | async-done | bytes 2621456 | tf_op jit(solution)/shard_map/reduce_scatter | solution.py:74
  213.5 2.2 convert_reduce_fusion
  215.7 0.5 fusion.45
  216.3 1.6 fusion.40
  218.0 0.5 all-gather.9.cloned.1.call-update
  218.6 37.1 %all-gather.7.cloned.1.call-done = bf16[4,1024,640]{2,1,0:T(8,128)(2,1)} async-done(((bf16[4,256,640]{2,1,0:T(8,128)(2,1)}), bf16[4,1024,640]{2,1,0:T(8,128)(2,1)}) %all-gather.7.cloned.1.call-update) | async-done | bytes 5242896 | tf_op jit(solution)/shard_map/all_gather | solution.py:77
  255.7 9.8 %multiply_convert_fusion.1 = (bf16[4,1024,640]{2,1,0:T(8,128)(2,1)}, f32[4,1024,640]{2,1,0:T(8,128)}) fusion(f32[640]{0:T(1024)S(1)} %copy-done.45, bf16[4,1024,640]{2,1,0:T(8,128)(2,1)} %all-gather.7.cloned.1.call-done, bf16[640,640]{1,0:T(8,128)(2,1)S(1)} %copy-done), kind=kOutput, calls=%fused_computation.19 | convolution fusion | flops 3371171840 | bytes 21793280 | tf_op jit(solution)/shard_map/bsd,df->bsf/dot_general | solution.py:78
  265.5 29.1 %all-gather.9.cloned.1.call-done = bf16[4,1024,640]{2,1,0:T(8,128)(2,1)} async-done(((bf16[4,256,640]{2,1,0:T(8,128)(2,1)}), bf16[4,1024,640]{2,1,0:T(8,128)(2,1)}) %all-gather.9.cloned.1.call-update) | async-done | bytes 5242896 | tf_op jit(solution)/shard_map/all_gather | solution.py:85
  294.6 11.3 %fusion.116 = (f32[640]{0:T(1024)}, bf16[4,1024,640]{2,1,0:T(8,128)(2,1)S(1)}) fusion(f32[4,1024,640]{2,1,0:T(8,128)} %get-tuple-element.70, f32[640]{0:T(1024)S(1)} %copy-done.45, bf16[4,1024,640]{2,1,0:T(8,128)(2,1)} %all-gather.9.cloned.1.call-done, bf16[640,640]{1,0:T(8,128)(2,1)S(1)} %copy-done.41), kind=kOutput, calls=%fused_computation.151 | convolution fusion | flops 3386899968 | bytes 21795840 | tf_op jit(solution)/shard_map/bsd,fd->bsf/dot_general | solution.py:88
  305.9 2.3 copy-done.46
  308.3 7.3 fusion.66
  315.7 9.6 %fusion.94 = f32[4,1024,640]{2,1,0:T(8,128)} fusion(bf16[4,1024,640]{2,1,0:T(8,128)(2,1)} %get-tuple-element.69, bf16[640,640]{1,0:T(8,128)(2,1)S(1)} %copy-done.41), kind=kOutput, calls=%fused_computation.113 | convolution fusion | flops 3355443200 | bytes 16547840 | tf_op jit(solution)/shard_map/bsf,fd->bsd/dot_general | solution.py:82
  325.3 68.3 %reduce-scatter.9.cloned.1.call-done = f32[4,256,640]{2,1,0:T(8,128)} async-done(((f32[4,1024,640]{2,1,0:T(8,128)}), f32[4,256,640]{2,1,0:T(8,128)}) %reduce-scatter.9.cloned.1.call-update) | async-done | bytes 2621456 | tf_op jit(solution)/shard_map/reduce_scatter | solution.py:94
  393.6 3.2 fusion.44
  396.9 77.1 %reduce-scatter.7.cloned.1.call-done = f32[4,256,640]{2,1,0:T(8,128)} async-done(((f32[4,1024,640]{2,1,0:T(8,128)}), f32[4,256,640]{2,1,0:T(8,128)}) %reduce-scatter.7.cloned.1.call-update) | async-done | bytes 2621456 | tf_op jit(solution)/shard_map/reduce_scatter | solution.py:83
  474.0 4.7 fusion.111
  478.7 1.5 copy-done.4
  480.2 1.2 convert_element_type.76
  481.4 0.2 reduce-scatter.11.cloned.1.call-start
  481.6 37.5 %all-gather.11.cloned.1.call-done = bf16[4,1024,640]{2,1,0:T(8,128)(2,1)} async-done(((bf16[4,256,640]{2,1,0:T(8,128)(2,1)}), bf16[4,1024,640]{2,1,0:T(8,128)(2,1)}) %all-gather.11.cloned.1.call-update) | async-done | bytes 5242896 | tf_op jit(solution)/shard_map/all_gather | solution.py:98
  519.1 4.3 fusion.74
  523.5 29.2 %fusion.71 = f32[1,4,1024,5,32]{2,4,3,1,0:T(8,128)} fusion(bf16[4,1024,5,32]{1,3,2,0:T(8,128)(2,1)S(1)} %fusion.74, f32[4,5,1024,1024]{2,3,1,0:T(8,128)} %get-tuple-element.68, f32[4,5,1024]{2,1,0:T(8,128)S(1)} %copy-done.23), kind=kOutput, calls=%fused_computation.99 | convolution fusion | flops 1384120320 | bytes 87900160 | tf_op jit(solution)/shard_map/bhqs,bqhk->bshk/dot_general | solution.py:101
  552.7 54.2 %multiply_reduce_fusion = (f32[4,5,1024]{2,1,0:T(8,128)S(1)}, f32[4,5,1024,1024]{2,3,1,0:T(8,128)}) fusion(f32[4,5,1024,1024]{2,3,1,0:T(8,128)} %get-tuple-element.68, f32[4,5,1024]{2,1,0:T(8,128)S(1)} %copy-done.23, bf16[4,1024,5,32]{1,3,2,0:T(8,128)(2,1)S(1)} %fusion.74, f32[3,4,1024,5,32]{2,4,3,0,1:T(8,128)} %copy-done.5), kind=kOutput, calls=%fused_computation.2 | convolution fusion | flops 1405071360 | bytes 170557440 | tf_op jit(solution)/shard_map/bqhk,bshk->bhqs/dot_general | solution.py:102
  606.9 65.3 %multiply_convert_fusion = bf16[4,5,1024,1024]{2,3,1,0:T(8,128)(2,1)} fusion(f32[4,5,1024,1024]{2,3,1,0:T(8,128)} %get-tuple-element.72, f32[4,5,1024]{2,1,0:T(8,128)S(1)} %get-tuple-element.71, f32[4,5,1024,1024]{2,3,1,0:T(8,128)} %get-tuple-element.68, f32[4,5,1024]{2,1,0:T(8,128)S(1)} %copy-done.23), kind=kLoop, calls=%fused_computation.1 | loop fusion | flops 83886080 | bytes 209879040 | tf_op jit(solution)/shard_map/convert_element_type | solution.py:103
  672.1 18.3 %fusion.117 = f32[4,5,32,1024]{3,2,1,0:T(8,128)S(1)} fusion(bf16[4,1024,5,32]{1,3,2,0:T(8,128)(2,1)} %copy-done.12, bf16[4,5,1024,1024]{2,3,1,0:T(8,128)(2,1)} %multiply_convert_fusion), kind=kOutput, calls=%fused_computation.152 | convolution fusion | flops 1342177280 | bytes 45875200 | tf_op jit(solution)/shard_map/bhqs,bqhk->bshk/dot_general | solution.py:105
  690.5 20.1 %bitcast_multiply_fusion.2 = (f32[4,1024,5,32]{1,3,2,0:T(8,128)}, f32[4,1024,5,32]{1,3,2,0:T(8,128)}, f32[4,5,32,1024]{3,2,1,0:T(8,128)}) fusion(f32[1024,32]{0,1:T(8,128)S(1)} %copy-done.15, f32[4,5,32,1024]{3,2,1,0:T(8,128)S(1)} %fusion.117, bf16[4,1024,5,32]{1,3,2,0:T(8,128)(2,1)} %get-tuple-element.48, bf16[4,5,1024,1024]{2,3,1,0:T(8,128)(2,1)} %multiply_convert_fusion), kind=kOutput, calls=%fused_computation.90 | convolution fusion | flops 1343488000 | bytes 53870592 | tf_op jit(solution)/shard_map/bhqs,bshk->bqhk/dot_general | solution.py:104
  710.5 2.1 fusion.113
  712.6 0.5 copy-done.6
  713.1 0.2 fusion.114
  713.3 1.5 copy-done.7
  714.8 1.6 fusion.62
  716.4 1.5 copy-done.8
  717.9 0.8 copy-done.10
  718.7 6.2 convolution_bitcast_fusion.1
  725.0 9.6 %convolution_bitcast_fusion.2 = f32[640,640]{1,0:T(8,128)} fusion(bf16[4,1024,640]{2,1,0:T(8,128)(2,1)} %get-tuple-element.69, bf16[4,1024,640]{2,1,0:T(8,128)(2,1)} %all-gather.9.cloned.1.call-done), kind=kOutput, calls=%fused_computation.103 | convolution fusion | flops 3355443200 | bytes 12124160 | tf_op jit(solution)/shard_map/bsf,bsd->fd/dot_general | solution.py:87
  734.7 8.1 fusion.80
  742.9 0.8 fusion.17
  743.7 0.6 copy.53
  744.3 2.0 fusion.90
  746.4 4.2 fusion.86
  750.7 52.3 %reduce-scatter.11.cloned.1.call-done = f32[4,256,640]{2,1,0:T(8,128)} async-done(((f32[4,1024,640]{2,1,0:T(8,128)}), f32[4,256,640]{2,1,0:T(8,128)}) %reduce-scatter.11.cloned.1.call-update) | async-done | bytes 2621456 | tf_op jit(solution)/shard_map/reduce_scatter | solution.py:111
  803.0 2.6 fusion.53
  805.7 10.1 %all-reduce = (f32[2,640]{1,0:T(2,128)S(1)}, f32[4,640]{1,0:T(4,128)S(1)}) all-reduce(f32[2,640]{1,0:T(2,128)S(1)} %pad_maximum_fusion.3, f32[4,640]{1,0:T(4,128)S(1)} %pad_maximum_fusion.2), channel_id=1, replica_groups=mesh['dp'=2,'tp'=4] {'tp'}, use_global_device_ids=true, to_apply=%region_17.18 | all-reduce | flops 3840 | bytes 30720 | tf_op jit(solution)/shard_map/psum | solution.py:112
  815.8 0.6 slice_reduce_fusion.4
  816.4 0.6 slice_reduce_fusion
  817.0 3.8 fusion.52
  (132 shorter events, 0.7 us)
Async XLA Ops:
  7.2 248.5 %copy-start = (bf16[640,640]{1,0:T(8,128)(2,1)S(1)}, bf16[640,640]{1,0:T(8,128)(2,1)}, u32[]{:S(2)}) copy-start(bf16[640,640]{1,0:T(8,128)(2,1)} %param.26) | copy-start | bytes 2457604
  7.2 4.3 copy-start.2
  7.2 4.3 copy-start.28
  7.2 4.3 copy-start.37
  7.2 46.5 %all-gather.5.cloned.1.call-start = ((), (), s32[]{:S(2)}) async-start(), calls=%async_computation.4 | async-start | bytes 6553600 | tf_op jit(solution)/shard_map/all_gather | solution.py:64
  9.0 1.9 copy-start.24
  9.0 4.2 copy-start.36
  9.0 5.3 copy-start.35
  9.0 44.7 %copy-start.42 = (bf16[3,640,5,32]{1,3,2,0:T(8,128)(2,1)S(1)}, bf16[3,640,5,32]{1,3,2,0:T(8,128)(2,1)}, u32[]{:S(2)}) copy-start(bf16[3,640,5,32]{1,3,2,0:T(8,128)(2,1)} %param.20) | copy-start | bytes 1843204
  10.9 0.6 copy-start.26
  13.2 200.3 %reduce-scatter.5.cloned.1.call-start = ((), (), s32[]{:S(2)}) async-start(), calls=%async_computation.5 | async-start | bytes 13107200 | tf_op jit(solution)/shard_map/reduce_scatter | solution.py:74
  59.0 3.7 copy-start.5
  59.8 2.9 copy-start.14
  59.8 2.9 copy-start.20
  59.8 2.9 copy-start.22
  65.1 35.3 %copy-start.12 = (bf16[4,1024,5,32]{1,3,2,0:T(8,128)(2,1)}, bf16[4,1024,5,32]{1,3,2,0:T(8,128)(2,1)S(1)}, u32[]{:S(2)}) copy-start(bf16[4,1024,5,32]{1,3,2,0:T(8,128)(2,1)S(1)} %get-tuple-element.49) | copy-start | bytes 3932164
  128.4 7.0 copy-start.18
  135.5 78.0 %copy-start.38 = (f32[640]{0:T(1024)S(1)}, f32[640]{0:T(1024)}, u32[]{:S(2)}) copy-start(f32[640]{0:T(1024)} %param.23) | copy-start | bytes 7684
  135.5 80.8 %copy-start.30 = (f32[640]{0:T(1024)S(1)}, f32[640]{0:T(1024)}, u32[]{:S(2)}) copy-start(f32[640]{0:T(1024)} %param.24) | copy-start | bytes 7684
  135.5 80.8 %copy-start.39 = (f32[640]{0:T(1024)S(1)}, f32[640]{0:T(1024)}, u32[]{:S(2)}) copy-start(f32[640]{0:T(1024)} %param.25) | copy-start | bytes 7684
  135.5 120.2 %all-gather.7.cloned.1.call-start = ((), (), s32[]{:S(2)}) async-start(), calls=%async_computation.6 | async-start | bytes 6553600 | tf_op jit(solution)/shard_map/all_gather | solution.py:77
  216.3 39.4 %copy-start.45 = (f32[640]{0:T(1024)S(1)}, f32[640]{0:T(1024)}, u32[]{:S(2)}) copy-start(f32[640]{0:T(1024)} %param.27) | copy-start | bytes 7684
  217.9 76.7 %all-gather.9.cloned.1.call-start = ((), (), s32[]{:S(2)}) async-start(), calls=%async_computation.8 | async-start | bytes 6553600 | tf_op jit(solution)/shard_map/all_gather | solution.py:85
  218.5 76.1 %copy-start.41 = (bf16[640,640]{1,0:T(8,128)(2,1)S(1)}, bf16[640,640]{1,0:T(8,128)(2,1)}, u32[]{:S(2)}) copy-start(bf16[640,640]{1,0:T(8,128)(2,1)} %param.28) | copy-start | bytes 2457604
  218.5 175.1 %reduce-scatter.9.cloned.1.call-start = ((), (), s32[]{:S(2)}) async-start(), calls=%async_computation.9 | async-start | bytes 13107200 | tf_op jit(solution)/shard_map/reduce_scatter | solution.py:94
  305.9 2.3 copy-start.46
  315.6 158.3 %reduce-scatter.7.cloned.1.call-start = ((), (), s32[]{:S(2)}) async-start(), calls=%async_computation.7 | async-start | bytes 13107200 | tf_op jit(solution)/shard_map/reduce_scatter | solution.py:83
  325.3 148.7 %copy-start.13 = (bf16[4,256,640]{2,1,0:T(8,128)(2,1)S(1)}, bf16[4,256,640]{2,1,0:T(8,128)(2,1)}, u32[]{:S(2)}) copy-start(bf16[4,256,640]{2,1,0:T(8,128)(2,1)} %param.16) | copy-start | bytes 3932164
  325.3 148.7 %copy-start.40 = (f32[640]{0:T(1024)S(1)}, f32[640]{0:T(1024)}, u32[]{:S(2)}) copy-start(f32[640]{0:T(1024)} %param.29) | copy-start | bytes 7684
  325.3 193.9 %all-gather.11.cloned.1.call-start = ((), (), s32[]{:S(2)}) async-start(), calls=%async_computation.10 | async-start | bytes 6553600 | tf_op jit(solution)/shard_map/all_gather | solution.py:98
  478.7 1.5 copy-start.4
  480.2 39.0 %copy-start.44 = (bf16[5,32,640]{2,1,0:T(8,128)(2,1)S(1)}, bf16[5,32,640]{2,1,0:T(8,128)(2,1)}, u32[]{:S(2)}) copy-start(bf16[5,32,640]{2,1,0:T(8,128)(2,1)} %param.22) | copy-start | bytes 614404
  481.4 42.1 %copy-start.23 = (f32[4,5,1024]{2,1,0:T(8,128)S(1)}, f32[4,5,1024]{2,1,0:T(8,128)}, u32[]{:S(2)}) copy-start(f32[4,5,1024]{2,1,0:T(8,128)} %get-tuple-element.67) | copy-start | bytes 245764
  481.4 321.5 %reduce-scatter.11.cloned.1.call-start = ((), (), s32[]{:S(2)}) async-start(), calls=%async_computation.11 | async-start | bytes 13107200 | tf_op jit(solution)/shard_map/reduce_scatter | solution.py:111
  672.1 18.3 %copy-start.15 = (f32[1024,32]{0,1:T(8,128)S(1)}, f32[1024,32]{0,1:T(8,128)}, u32[]{:S(2)}) copy-start(f32[1024,32]{0,1:T(8,128)} %get-tuple-element.66) | copy-start | bytes 393220
  710.5 2.5 copy-start.6
  713.1 1.7 copy-start.7
  713.1 1.7 copy-start.21
  714.8 3.9 copy-start.16
  714.8 3.9 copy-start.43
  716.4 1.5 copy-start.8
  716.4 2.3 copy-start.10
  724.9 9.7 %slice-start.4 = ((s8[5242880]{0:T(1024)(128)(4,1)}), s8[1048576]{0:T(1024)(128)(4,1)S(1)}, s32[]{:S(2)}) async-start(s8[5242880]{0:T(1024)(128)(4,1)} %bitcast.140), calls=%async_computation.16 | async-start | bytes 2097152
  724.9 9.7 %slice-start.5 = ((s8[5242880]{0:T(1024)(128)(4,1)}), s8[4194304]{0:T(1024)(128)(4,1)S(1)}, s32[]{:S(2)}) async-start(s8[5242880]{0:T(1024)(128)(4,1)} %bitcast.140), calls=%async_computation.17 | async-start | bytes 8388608
  725.0 19.4 %slice-start = ((s8[5242880]{0:T(1024)(128)(4,1)}), s8[4194304]{0:T(1024)(128)(4,1)S(1)}, s32[]{:S(2)}) async-start(s8[5242880]{0:T(1024)(128)(4,1)} %bitcast.136), calls=%async_computation.12 | async-start | bytes 8388608
  734.6 8.2 copy-start.32
  734.6 8.2 copy-start.31
  734.6 8.2 copy-start.34
  734.6 8.2 copy-start.33
  734.7 8.2 copy-start.9
  734.7 8.2 copy-start.11
  734.7 8.2 copy-start.17
  734.7 9.7 %slice-start.1 = ((s8[5242880]{0:T(1024)(128)(4,1)}), s8[1048576]{0:T(1024)(128)(4,1)S(1)}, s32[]{:S(2)}) async-start(s8[5242880]{0:T(1024)(128)(4,1)} %bitcast.136), calls=%async_computation.13 | async-start | bytes 2097152
  734.7 11.7 %slice-start.2 = ((s8[5242880]{0:T(1024)(128)(4,1)}), s8[4194304]{0:T(1024)(128)(4,1)S(1)}, s32[]{:S(2)}) async-start(s8[5242880]{0:T(1024)(128)(4,1)} %bitcast.138), calls=%async_computation.14 | async-start | bytes 8388608
  742.9 1.4 copy-start.19
  742.9 3.4 slice-start.3
  746.4 56.6 %copy-start.3 = (bf16[4,256,640]{2,1,0:T(8,128)(2,1)S(1)}, bf16[4,256,640]{2,1,0:T(8,128)(2,1)}, u32[]{:S(2)}) copy-start(bf16[4,256,640]{2,1,0:T(8,128)(2,1)} %param.15) | copy-start | bytes 3932164
  746.4 56.6 %copy-start.25 = (f32[4,256]{1,0:T(4,128)S(1)}, f32[4,256]{1,0:T(4,128)}, u32[]{:S(2)}) copy-start(f32[4,256]{1,0:T(4,128)} %copy-done.24) | copy-start | bytes 12292
  746.4 56.6 %copy-start.27 = (f32[4,256]{1,0:T(4,128)S(1)}, f32[4,256]{1,0:T(4,128)}, u32[]{:S(2)}) copy-start(f32[4,256]{1,0:T(4,128)} %copy-done.26) | copy-start | bytes 12292
  746.4 56.6 %copy-start.29 = (f32[640]{0:T(1024)S(1)}, f32[640]{0:T(1024)}, u32[]{:S(2)}) copy-start(f32[640]{0:T(1024)} %param.18) | copy-start | bytes 7684
  816.4 4.5 copy-start.1
Sparse Core Ops, SparseCore 0:
  13.3 40.3 all-gather.4
  135.6 77.8 reduce-scatter.4
  218.0 37.5 all-gather.6
  257.0 37.5 all-gather.8
  315.7 77.8 reduce-scatter.8
  396.0 77.8 reduce-scatter.6
  481.5 37.5 all-gather.10
  725.1 77.8 reduce-scatter.10
where the time goes:
time: 837 us; the launch traced here: 828 us
  waiting for transfers between devices  419 us (50%)
  matrix products  270 us (32%)
  other arithmetic  100 us (12%)
  between operations  15.2 us (2%)
  local copies, waits for them, and re-layouts  13 us (2%)
  blocking collectives  10.1 us (1%)
    reduce_scatter x1, waiting for transfers between devices, device_step(): lax.psum_scatter(attn_part, 'tp', scatter_dimension=1, tiled=True)  77.6 us
    reduce_scatter x1, waiting for transfers between devices, device_step(): mlp_sum = lax.psum_scatter(mlp_part, 'tp', scatter_dimension=1, tiled=True)  77.1 us
    reduce_scatter x1, waiting for transfers between devices, device_step(): d_h2 = lax.psum_scatter(d_h2_part, 'tp', scatter_dimension=1, tiled=True)  68.3 us
    convert_element_type x1, other arithmetic, device_step(): (attn_probs * (d_probs - jnp.sum(d_probs * attn_probs, axis=-1, keepdims=...  65.3 us
    dot_general x1, matrix products, device_step(): jnp.einsum('bqhk,bshk->bhqs', d_attn_o, v_heads, preferred_element_type=j...  54.2 us
    reduce_scatter x1, waiting for transfers between devices, device_step(): d_h1 = lax.psum_scatter(d_h1_part, 'tp', scatter_dimension=1, tiled=True)  52.3 us
    all_gather x1, waiting for transfers between devices, device_step(): lax.all_gather(h1_f.astype(jnp.bfloat16), 'tp', axis=1, tiled=True)  39.4 us
    all_gather x1, waiting for transfers between devices, device_step(): lax.all_gather(d_x1.astype(jnp.bfloat16), 'tp', axis=1, tiled=True)  37.5 us
  transfers between devices with their start and end apart: 8, of which 8 were waited for; matrix products, arithmetic and copies ran while one was open for 6% of the time, Pallas kernels for 0%

commit v1 on v0

v1 whole, which is shorter than its diff:
```python
import functools

import jax
import jax.numpy as jnp
from jax import lax
from jax.experimental import pallas as pl
from jax.experimental.pallas import tpu as pltpu
from jax.sharding import PartitionSpec as P

LN_EPS = 1e-5
ROPE_BASE = 10000.0
INV_SQRT2 = 0.7071067811865476
INV_SQRT_2PI = 0.3989422804014327
NEG_LARGE = -1e30
F32 = jnp.float32
BF16 = jnp.bfloat16
KEY_STEP = 256


def dot(lhs, rhs):
    return jnp.dot(lhs, rhs, preferred_element_type=F32)


def layer_norm(values, ln_gain, ln_bias):
    centered = values - jnp.mean(values, axis=-1, keepdims=True)
    inv_std = lax.rsqrt(jnp.mean(centered * centered, axis=-1, keepdims=True) + LN_EPS)
    x_hat = centered * inv_std
    return x_hat * ln_gain + ln_bias, x_hat, inv_std


def layer_norm_grad(d_out, x_hat, inv_std, ln_gain):
    d_hat = d_out * ln_gain
    return inv_std * (d_hat - jnp.mean(d_hat, axis=-1, keepdims=True) - x_hat * jnp.mean(d_hat * x_hat, axis=-1, keepdims=True))


def rope_tables(seq_len, head_dim):
    half_dim = head_dim // 2
    inv_freq = ROPE_BASE ** (-2.0 * jnp.arange(half_dim, dtype=F32) / head_dim)
    angles = inv_freq[:, None] * jnp.arange(seq_len, dtype=F32)[None, :]
    angles = jnp.concatenate([angles, angles], axis=0)
    return jnp.cos(angles), jnp.sin(angles)


def rotate(tensor, cos_tab, sin_tab):
    half_dim = tensor.shape[-2] // 2
    swapped = jnp.concatenate([-tensor[..., half_dim:, :], tensor[..., :half_dim, :]], axis=-2)
    return tensor * cos_tab + swapped * sin_tab


def rotate_back(grad_in, cos_tab, sin_tab):
    half_dim = grad_in.shape[-2] // 2
    scaled = grad_in * sin_tab
    swapped = jnp.concatenate([scaled[..., half_dim:, :], -scaled[..., :half_dim, :]], axis=-2)
    return grad_in * cos_tab + swapped


def masked_scores(k_ref, q, length, keys):
    scores = dot(k_ref[0, :, :keys].T, q)
    tail = keys - KEY_STEP
    rows = lax.broadcasted_iota(jnp.int32, (KEY_STEP, scores.shape[1]), 0) + tail
    last = jnp.where(rows < length, scores[tail:], NEG_LARGE)
    return last if tail == 0 else jnp.concatenate([scores[:tail], last], axis=0)


def for_key_count(length, seq_len, body):
    blocks = lax.div(length + KEY_STEP - 1, KEY_STEP)
    for count in range(1, seq_len // KEY_STEP + 1):
        pl.when(blocks == count)(functools.partial(body, count * KEY_STEP))


def attn_fwd_kernel(len_ref, q_ref, k_ref, v_ref, o_ref, o_wide_ref, lse_ref):
    length = len_ref[0]

    def body(keys):
        scores = masked_scores(k_ref, q_ref[0], length, keys)
        top = jnp.max(scores, axis=0, keepdims=True)
        weights = jnp.exp(scores - top)
        total = jnp.sum(weights, axis=0, keepdims=True)
        out = dot(v_ref[0, :, :keys], weights.astype(BF16)) / total
        o_ref[0] = out.astype(BF16)
        o_wide_ref[0] = out
        lse_ref[0] = top + jnp.log(total)

    for_key_count(length, q_ref.shape[-1], body)


def attn_bwd_kernel(len_ref, q_ref, k_ref, v_ref, do_ref, o_wide_ref, lse_ref, dq_ref, dk_ref, dv_ref):
    length = len_ref[0]
    dk_ref[...] = jnp.zeros_like(dk_ref)
    dv_ref[...] = jnp.zeros_like(dv_ref)

    def body(keys):
        q, d_out = q_ref[0], do_ref[0]
        delta = jnp.sum(d_out.astype(F32) * o_wide_ref[0], axis=0, keepdims=True)
        probs = jnp.exp(masked_scores(k_ref, q, length, keys) - lse_ref[0])
        d_probs = dot(v_ref[0, :, :keys].T, d_out)
        d_scores = (probs * (d_probs - delta)).astype(BF16)
        dv_ref[0, :, :keys] = dot(probs.astype(BF16), d_out.T).T
        dk_ref[0, :, :keys] = dot(d_scores, q.T).T
        dq_ref[0] = dot(k_ref[0, :, :keys], d_scores)

    for_key_count(length, q_ref.shape[-1], body)


def head_call(kernel, name, length, ins, outs, cost):
    heads = ins[0].shape[0]

    def spec(array):
        return pl.BlockSpec((1,) + array.shape[1:], lambda head, *_: (head, 0, 0))

    return pl.pallas_call(
        kernel,
        grid_spec=pltpu.PrefetchScalarGridSpec(num_scalar_prefetch=1, grid=(heads,), in_specs=[spec(a) for a in ins], out_specs=[spec(a) for a in outs]),
        out_shape=outs,
        compiler_params=pltpu.CompilerParams(vmem_limit_bytes=40 << 20),
        cost_estimate=pl.CostEstimate(flops=cost, bytes_accessed=1 << 24, transcendentals=1 << 24),
        name=name,
    )(length, *ins)


def solution(mesh):
    tp = mesh.shape['tp']
    act_spec = P('dp', 'tp', None)
    rep_vec = P(None)
    part_vec = P('dp')
    in_specs = (act_spec, act_spec, P('dp', None), rep_vec, rep_vec, P(None, None, 'tp', None), P(None, 'tp', None),
                P('tp', None, None), rep_vec, rep_vec, rep_vec, P(None, 'tp'), P('tp'), P('tp', None), rep_vec)
    out_specs = (act_spec, act_spec, part_vec, part_vec, P('dp', None, 'tp', None), P('dp', 'tp', None),
                 P(('dp', 'tp'), None, None), part_vec, part_vec, part_vec, P('dp', 'tp'), P(('dp', 'tp')),
                 P(('dp', 'tp'), None), part_vec)

    def swap(value, mask):
        return lax.ppermute(value, 'tp', [(i, i ^ mask) for i in range(tp)])

    def to_sequence(local, me):
        chunk, width = local.shape[1:]
        full = jnp.zeros((tp * chunk, width), local.dtype)
        for mask in range(tp):
            other = me ^ mask
            piece = lax.dynamic_index_in_dim(local, other, 0, keepdims=False)
            piece = swap(piece, mask) if mask else piece
            full = lax.dynamic_update_slice(full, piece, (other * chunk, 0))
        return full

    def from_sequence(full, me):
        rows, width = full.shape
        chunk = rows // tp
        local = jnp.zeros((tp, chunk, width), full.dtype)
        for mask in range(tp):
            other = me ^ mask
            piece = lax.dynamic_slice(full, (other * chunk, 0), (chunk, width))
            piece = swap(piece, mask) if mask else piece
            local = lax.dynamic_update_slice(local, piece[None], (other, 0, 0))
        return local

    def gather(shard):
        far = swap(shard, 2)
        near = swap(jnp.stack([shard, far]), 1)
        return jnp.stack([shard, near[0], far, near[1]])

    def scatter_sum(parts):
        near = jnp.stack([parts[0], parts[2]]) + swap(jnp.stack([parts[1], parts[3]]), 1)
        return near[0] + swap(near[1], 2)

    def all_sum(value):
        value = value + swap(value, 1)
        return value + swap(value, 2)

    def device_step(x_in, grad_y, pad_mask, ln1_gain, ln1_bias, w_qkv, b_qkv, w_out, b_out, ln2_gain, ln2_bias, w_up, b_up, w_down, b_down):
        me = lax.axis_index('tp')
        seq_len = pad_mask.shape[1]
        local_heads, head_dim = w_qkv.shape[2:]
        width = x_in.shape[2]
        heads = local_heads * tp
        q_scale = head_dim ** -0.5
        cos_tab, sin_tab = rope_tables(seq_len, head_dim)
        length = jnp.sum((lax.dynamic_index_in_dim(pad_mask, me, 0) > 0).astype(jnp.int32), axis=1)
        x_f = to_sequence(x_in, me).astype(F32)
        qkv_rows = 3 * local_heads * head_dim
        wq_all = gather(w_qkv.transpose(0, 2, 3, 1).reshape(qkv_rows, width)).reshape(tp * qkv_rows, width)
        bq_all = gather(b_qkv.reshape(1, qkv_rows)).reshape(tp, 3, local_heads, head_dim)
        h1_f, x_hat1, inv_std1 = layer_norm(x_f, ln1_gain, ln1_bias)
        h1 = h1_f.astype(BF16)
        qkv_all = lax.dot_general(wq_all, h1, (((1,), (1,)), ((), ())), preferred_element_type=F32)
        qkv_all = qkv_all.reshape(tp, 3, local_heads, head_dim, seq_len) + bq_all[..., None]

        def by_head(value):
            return value.reshape(heads, head_dim, seq_len)

        q_rot = by_head(rotate(qkv_all[:, 0] * q_scale, cos_tab, sin_tab).astype(BF16))
        k_rot = by_head(rotate(qkv_all[:, 1], cos_tab, sin_tab).astype(BF16))
        v_heads = by_head(qkv_all[:, 2].astype(BF16))
        head_bf16 = jax.ShapeDtypeStruct((heads, head_dim, seq_len), BF16)
        head_f32 = jax.ShapeDtypeStruct((heads, head_dim, seq_len), F32)
        head_row = jax.ShapeDtypeStruct((heads, 1, seq_len), F32)
        attn_o, attn_wide, lse = head_call(attn_fwd_kernel, 'attn_fwd', length, (q_rot, k_rot, v_heads), (head_bf16, head_f32, head_row), 30 * 10 ** 9)
        wo_all = gather(w_out.reshape(local_heads * head_dim, width)).reshape(heads * head_dim, width)
        wu_all = gather(w_up)
        bu_all = gather(b_up)
        wd_all = gather(w_down)
        dy_full = to_sequence(grad_y, me)
        attn_sum = lax.dot_general(attn_o.reshape(heads * head_dim, seq_len), wo_all, (((0,), (0,)), ((), ())), preferred_element_type=F32) + b_out
        x1_f = (x_f + attn_sum).astype(BF16).astype(F32)
        h2_f, x_hat2, inv_std2 = layer_norm(x1_f, ln2_gain, ln2_bias)
        h2 = h2_f.astype(BF16)
        pre_act = jnp.einsum('sd,mdf->msf', h2, wu_all, preferred_element_type=F32) + bu_all[:, None, :]
        erf_term = lax.erf(pre_act * INV_SQRT2)
        act_b = (0.5 * pre_act * (1.0 + erf_term)).astype(BF16)
        gelu_slope = 0.5 * (1.0 + erf_term) + pre_act * jnp.exp(-0.5 * pre_act * pre_act) * INV_SQRT_2PI
        mlp_sum = jnp.einsum('msf,mfd->sd', act_b, wd_all, preferred_element_type=F32) + b_down
        y_out = from_sequence((x1_f + mlp_sum).astype(BF16), me)
        dy_f = dy_full.astype(F32)
        d_pre = jnp.einsum('sd,mfd->msf', dy_full, wd_all, preferred_element_type=F32) * gelu_slope
        d_pre_b = d_pre.astype(BF16)
        d_h2 = jnp.einsum('msf,mdf->sd', d_pre_b, wu_all, preferred_element_type=F32)
        d_x1 = dy_f + layer_norm_grad(d_h2, x_hat2, inv_std2, ln2_gain)
        d_x1_b = d_x1.astype(BF16)
        d_attn = lax.dot_general(wo_all, d_x1_b, (((1,), (1,)), ((), ())), preferred_element_type=F32).astype(BF16).reshape(heads, head_dim, seq_len)
        grad_w_down = scatter_sum(jnp.einsum('msf,sd->mfd', act_b, dy_full, preferred_element_type=F32))
        grad_w_up = scatter_sum(jnp.einsum('sd,msf->mdf', h2, d_pre_b, preferred_element_type=F32))
        grad_w_out = scatter_sum(jnp.einsum('ms,sd->md', attn_o.reshape(heads * head_dim, seq_len), d_x1_b, preferred_element_type=F32).reshape(tp, local_heads * head_dim, width))
        grad_b_up = scatter_sum(jnp.sum(d_pre, axis=1))
        mid_sums = all_sum(jnp.stack([jnp.sum(dy_f, axis=0), jnp.sum(d_h2 * x_hat2, axis=0), jnp.sum(d_h2, axis=0), jnp.sum(d_x1, axis=0)]))
        d_query, d_key, d_value = head_call(attn_bwd_kernel, 'attn_bwd', length, (q_rot, k_rot, v_heads, d_attn, attn_wide, lse), (head_f32,) * 3, 60 * 10 ** 9)

        def by_shard(value):
            return value.reshape(tp, local_heads, head_dim, seq_len)

        d_qkv = jnp.stack([by_shard(rotate_back(d_query, cos_tab, sin_tab) * q_scale), by_shard(rotate_back(d_key, cos_tab, sin_tab)), by_shard(d_value)], axis=1)
        grad_b_qkv = scatter_sum(jnp.sum(d_qkv, axis=-1).reshape(tp, qkv_rows)).reshape(3, local_heads, head_dim)
        d_qkv_b = d_qkv.astype(BF16).reshape(tp * qkv_rows, seq_len)
        d_h1 = lax.dot_general(d_qkv_b, wq_all, (((0,), (0,)), ((), ())), preferred_element_type=F32)
        grad_w_qkv = scatter_sum(dot(d_qkv_b, h1).reshape(tp, qkv_rows, width))
        grad_w_qkv = grad_w_qkv.reshape(3, local_heads, head_dim, width).transpose(0, 3, 1, 2)
        ln1_sums = all_sum(jnp.stack([jnp.sum(d_h1 * x_hat1, axis=0), jnp.sum(d_h1, axis=0)]))
        grad_x = from_sequence((d_x1 + layer_norm_grad(d_h1, x_hat1, inv_std1, ln1_gain)).astype(BF16), me)
        grad_w_out = grad_w_out.reshape(local_heads, head_dim, width)
        return (y_out, grad_x, ln1_sums[0], ln1_sums[1], grad_w_qkv, grad_b_qkv, grad_w_out, mid_sums[3],
                mid_sums[1], mid_sums[2], grad_w_up, grad_b_up, grad_w_down, mid_sums[0])

    return jax.shard_map(device_step, mesh=mesh, in_specs=in_specs, out_specs=out_specs, check_vma=False)
```

time: 837 us -> 502 us (0.60)
  waiting for transfers between devices: 419 us -> 166 us
  matrix products: 270 us -> 64.5 us
  Pallas kernels: 0 us -> 90.6 us
  local copies, waits for them, and re-layouts: 13 us -> 86.3 us
  other arithmetic: 100 us -> 63.1 us
  starting transfers between devices: 0.84 us -> 19.6 us
  between operations: 15.2 us -> 2.51 us
  blocking collectives: 10.1 us -> 0 us
    reduce_scatter x4 -> x0, waiting for transfers between devices: 275 us -> none  [the longest x1 77.6 us: device_step(): lax.psum_scatter(attn_part, 'tp', scatter_dimension=1, tiled=True)]
    dot_general x17 -> x12, matrix products: 235 us -> 64.5 us  [the longest x1 9.9 us: device_step(): jnp.einsum('sd,msf->mdf', h2, d_pre_b, preferred_element_type=F32)]
    ppermute x0 -> x40, waiting for transfers between devices: none -> 166 us  [swap(): return lax.ppermute(value, 'tp', [(i, i ^ mask) for i in range(tp)])]
    all_gather x4 -> x0, waiting for transfers between devices: 143 us -> none  [the longest x1 39.4 us: device_step(): lax.all_gather(h1_f.astype(jnp.bfloat16), 'tp', axis=1, tiled=True)]
    pallas_call x0 -> x2, Pallas kernels: none -> 90.6 us  [head_call(): pl.pallas_call(kernel, grid_spec=pltpu.PrefetchScalarGridSpec(num_scalar_...]
    convert_element_type x6 -> x3, other arithmetic: 75.9 us -> 6.35 us  [the longest x1 2.58 us: device_step(): (d_x1 + layer_norm_grad(d_h1, x_hat1, inv_std1, ln1_gain)).astype(BF16)]
    sub x1 -> x0, matrix products: 35.2 us -> none  [device_step(): attn_probs = jax.nn.softmax(jnp.where(key_ok, scores, NEG_LARGE), axis=-1)]
    ppermute x0 -> x40, starting transfers between devices: none -> 19.6 us  [swap(): return lax.ppermute(value, 'tp', [(i, i ^ mask) for i in range(tp)])]
  transfers between devices with their start and end apart: 8 -> 40, of which waited for: 8 -> 13; matrix products, arithmetic and copies ran while one was open for 6% -> 24% of each run, Pallas kernels for 0% -> 7%
where the time goes in v1:
time: 502 us; the launch traced here: 492 us
  waiting for transfers between devices  166 us (33%)
  Pallas kernels  90.6 us (18%)
  local copies, waits for them, and re-layouts  86.3 us (17%)
  matrix products  64.5 us (13%)
  other arithmetic  63.1 us (13%)
  starting transfers between devices  19.6 us (4%)
    ppermute x40, waiting for transfers between devices, swap(): return lax.ppermute(value, 'tp', [(i, i ^ mask) for i in range(tp)])  166 us
    pallas_call x2, Pallas kernels, head_call(): pl.pallas_call(kernel, grid_spec=pltpu.PrefetchScalarGridSpec(num_scalar_...  90.6 us
    ppermute x40, starting transfers between devices, swap(): return lax.ppermute(value, 'tp', [(i, i ^ mask) for i in range(tp)])  19.6 us
    unnamed x172, local copies, waits for them, and re-layouts  13.9 us
    slice x7, local copies, waits for them, and re-layouts, scatter_sum(): parts[0]  12.2 us
    dynamic_slice x9, local copies, waits for them, and re-layouts, to_sequence(): piece = lax.dynamic_index_in_dim(local, other, 0, keepdims=False)  11.4 us
    broadcast_in_dim x6, local copies, waits for them, and re-layouts, from_sequence(): local = lax.dynamic_update_slice(local, piece[None], (other, 0, 0))  11.4 us
    add x6, other arithmetic, scatter_sum(): return near[0] + swap(near[1], 2)  10.5 us
  transfers between devices with their start and end apart: 40, of which 13 were waited for; matrix products, arithmetic and copies ran while one was open for 24% of the time, Pallas kernels for 7%

profile of v1, /device:TPU:0, one launch (start us, length us, event | category | flops | bytes accessed | tf_op | source)
XLA Modules:
  0.0 492.3 jit_solution(5900979866109722571)
XLA Ops:
  2.0 3.3 collective-permute-start.5
  5.4 2.7 constant_dynamic-slice_fusion.4
  9.9 2.0 collective-permute-start.1
  14.9 1.8 copy.68
  16.7 1.9 copy.78
  18.6 1.9 copy.79
  20.4 1.9 copy.80
  26.5 2.4 collective-permute-done.11
  31.2 7.9 %collective-permute-done.7 = bf16[160,640]{1,0:T(8,128)(2,1)S(1)} collective-permute-done((bf16[160,640]{1,0:T(8,128)(2,1)}, bf16[160,640]{1,0:T(8,128)(2,1)S(1)}, u32[]{:S(2)}, u32[]{:S(2)}) %collective-permute-start.7) | collective-permute-done | bytes 204832 | tf_op jit(solution)/shard_map/ppermute | solution.py:133
  49.6 35.3 %collective-permute-done.19 = bf16[256,640]{0,1:T(8,128)(2,1)S(1)} collective-permute-done((bf16[256,640]{0,1:T(8,128)(2,1)}, bf16[256,640]{0,1:T(8,128)(2,1)S(1)}, u32[]{:S(2)}, u32[]{:S(2)}) %collective-permute-start.19) | collective-permute-done | bytes 327712 | tf_op jit(solution)/shard_map/ppermute | solution.py:133
  84.9 4.4 collective-permute-done.20
  94.3 4.9 broadcast_add_fusion
  104.0 34.4 %attn_fwd.1 = (bf16[20,32,1024]{2,1,0:T(8,128)(2,1)S(1)}, f32[20,32,1024]{2,1,0:T(8,128)S(1)}, f32[20,1,1024]{2,1,0:T(1,128)S(1)}) custom-call(s32[1]{0:T(128)} %bitcast.4.len_ref, bf16[20,32,1024]{2,1,0:T(8,128)(2,1)S(1)} %get-tuple-element.130.q_ref, bf16[20,32,1024]{2,1,0:T(8,128)(2,1)S(1)} %get-tuple-element.129.k_ref, bf16[20,32,1024]{2,1,0:T(8,128)(2,1)S(1)} %bitcast.179), custom_call_target="tpu_custom_call" | custom-call | flops 30000001024 | bytes 16777216 | tf_op jit(solution)/shard_map/attn_fwd/pallas_call | solution.py:111
  138.5 3.5 pad_maximum_fusion.5
  143.9 1.8 fusion.94
  145.8 8.2 %fusion.6 = (bf16[4,1024,640]{1,2,0:T(8,128)(2,1)}, f32[4,640,1024]{2,1,0:T(8,128)S(1)}) fusion(f32[4,640]{1,0:T(4,128)S(1)} %pad_maximum_fusion.18, bf16[1024,640]{0,1:T(8,128)(2,1)S(1)} %get-tuple-element.149, f32[640]{0:T(1024)S(1)} %copy-done.75, f32[640]{0:T(1024)S(1)} %copy-done.72, f32[1024]{0:T(1024)S(1)} %add_rsqrt_fusion, ...), kind=kOutput, calls=%fused_computation.9 | convolution fusion | flops 3380019200 | bytes 20339712 | tf_op jit(solution)/shard_map/sd,mdf->msf/dot_general | solution.py:206
  154.0 1.7 fusion.93
  156.2 8.6 %fusion.103 = (f32[4,640]{1,0:T(4,128)S(1)}, bf16[4,1024,640]{1,2,0:T(8,128)(2,1)S(1)}) fusion(f32[4,640,1024]{2,1,0:T(8,128)S(1)} %get-tuple-element.151, f32[4,640]{1,0:T(4,128)S(1)} %pad_maximum_fusion.18, bf16[1024,640]{0,1:T(8,128)(2,1)S(1)} %copy-done.23, bf16[1,640,640]{2,1,0:T(8,128)(2,1)S(1)} %get-tuple-element.101, ...), kind=kOutput, calls=%fused_computation.229 | convolution fusion | flops 3391813120 | bytes 20336640 | tf_op jit(solution)/shard_map/sd,mfd->msf/dot_general | solution.py:213
  164.9 6.0 %fusion.102 = (f32[640]{0:T(1024)S(1)}, f32[1024,640]{1,0:T(8,128)}) fusion(bf16[1,640,640]{1,2,0:T(8,128)(2,1)S(1)} %get-tuple-element.103, bf16[1,640,640]{1,2,0:T(8,128)(2,1)S(1)} %bitcast.220, bf16[1,640,640]{1,2,0:T(8,128)(2,1)S(1)} %get-tuple-element.102, bf16[1,640,640]{1,2,0:T(8,128)(2,1)S(1)} %bitcast.198, ...), kind=kOutput, calls=%fused_computation.228 | convolution fusion | flops 3361013248 | bytes 11143680 | tf_op jit(solution)/shard_map/msf,mdf->sd/dot_general | solution.py:215
  170.9 3.3 copy.84
  174.2 3.1 fusion.28
  177.4 3.0 fusion.87
  182.7 56.2 %attn_bwd.1 = (f32[20,32,1024]{2,1,0:T(8,128)S(1)}, f32[20,32,1024]{2,1,0:T(8,128)S(1)}, f32[20,32,1024]{2,1,0:T(8,128)S(1)}) custom-call(s32[1]{0:T(128)} %bitcast.4.len_ref, bf16[20,32,1024]{2,1,0:T(8,128)(2,1)S(1)} %get-tuple-element.130.q_ref, bf16[20,32,1024]{2,1,0:T(8,128)(2,1)S(1)} %get-tuple-element.129.k_ref, bf16[20,32,1024]{2,1,0:T(8,128)(2,1)S(1)} %bitcast.180, ...), custom_call_target="tpu_custom_call" | custom-call | flops 60000002048 | bytes 16777216 | tf_op jit(solution)/shard_map/attn_bwd/pallas_call | solution.py:111
  239.7 1.8 fusion.92
  241.5 3.3 fusion.45
  244.8 2.3 fusion.10
  249.7 9.9 %convolution_bitcast_fusion = f32[4,640,640]{1,2,0:T(8,128)} fusion(bf16[4,1024,640]{1,2,0:T(8,128)(2,1)} %copy-done.79, bf16[1024,640]{0,1:T(8,128)(2,1)S(1)} %copy-done.15, f32[640]{0:T(1024)S(1)} %copy-done.75, f32[640]{0:T(1024)S(1)} %copy-done.72, f32[1024]{0:T(1024)S(1)} %add_rsqrt_fusion, f32[1024]{0:T(1024)S(1)} %broadcast_multiply_fusion.7), kind=kOutput, calls=%fused_computation.42 | convolution fusion | flops 3359375360 | bytes 13120512 | tf_op jit(solution)/shard_map/sd,msf->mdf/dot_general | solution.py:220
  259.7 6.5 %fusion.62 = f32[4,640,640]{2,1,0:T(8,128)} fusion(bf16[4,1024,640]{1,2,0:T(8,128)(2,1)S(1)} %bitcast.235, bf16[1024,640]{0,1:T(8,128)(2,1)S(1)} %copy-done.24), kind=kOutput, calls=%fused_computation.105 | convolution fusion | flops 3355443200 | bytes 13107200 | tf_op jit(solution)/shard_map/msf,sd->mfd/dot_general | solution.py:219
  266.2 3.9 fusion.40
  272.2 7.8 %fusion.84 = f32[1920,640]{1,0:T(8,128)} fusion(bf16[1920,1024]{1,0:T(8,128)(2,1)} %bitcast.194, bf16[1024,640]{0,1:T(8,128)(2,1)S(1)} %copy-done.7, f32[640]{0:T(1024)S(1)} %copy-done.78, f32[640]{0:T(1024)S(1)} %copy-done.71, f32[1024]{0:T(1024)S(1)} %copy-done.69, f32[1024]{0:T(1024)S(1)} %copy-done.67), kind=kOutput, calls=%fused_computation.212 | convolution fusion | flops 2520514560 | bytes 10171392 | tf_op jit(solution)/shard_map/dot_general | solution.py:21
  280.0 5.0 %fusion.101 = (f32[640]{0:T(1024)S(1)}, f32[1024,640]{1,0:T(8,128)}) fusion(bf16[1920,1024]{1,0:T(8,128)(2,1)S(1)} %bitcast.195, bf16[1920,640]{1,0:T(8,128)(2,1)S(1)} %bitcast.199), kind=kOutput, calls=%fused_computation.227 | convolution fusion | flops 2517237248 | bytes 9013760 | tf_op jit(solution)/shard_map/dot_general | solution.py:232
  285.0 3.5 copy.88
  288.5 2.8 fusion.37
  291.3 2.6 fusion.36
  296.0 3.7 slice_bitcast_fusion.9
  303.1 5.2 %fusion.90 = (f32[1,640,640]{1,2,0:T(8,128)}, f32[1,640,640]{1,2,0:T(8,128)S(1)}, f32[1,640,640]{1,2,0:T(8,128)S(1)}, f32[1,640,640]{1,2,0:T(8,128)}) fusion(f32[4,640,640]{1,2,0:T(8,128)} %convolution_bitcast_fusion), kind=kLoop, calls=%fused_computation.216 | loop fusion | bytes 13107200 | tf_op jit(solution)/shard_map/slice | solution.py:162
  308.3 1.9 pad_maximum_fusion.3
  310.8 2.2 fusion.89
  316.1 2.0 pad_maximum_fusion.4
  319.0 3.5 collective-permute-done.29
  322.5 3.6 collective-permute-done.37
  326.1 3.6 collective-permute-done.25
  334.6 6.6 %collective-permute-done.16 = bf16[256,640]{0,1:T(8,128)(2,1)S(1)} collective-permute-done((bf16[256,640]{0,1:T(8,128)(2,1)S(1)}, bf16[256,640]{0,1:T(8,128)(2,1)S(1)}, u32[]{:S(2)}, u32[]{:S(2)}) %collective-permute-start.16) | collective-permute-done | bytes 327712 | tf_op jit(solution)/shard_map/ppermute | solution.py:133
  341.9 1.9 copy.74
  343.8 2.0 copy.75
  345.8 5.4 %collective-permute-done.17 = bf16[256,640]{0,1:T(8,128)(2,1)} collective-permute-done((bf16[256,640]{0,1:T(8,128)(2,1)}, bf16[256,640]{0,1:T(8,128)(2,1)}, u32[]{:S(2)}, u32[]{:S(2)}) %collective-permute-start.17) | collective-permute-done | bytes 327712 | tf_op jit(solution)/shard_map/ppermute | solution.py:133
  351.4 1.9 copy.76
  353.3 1.7 constant_dynamic-update-slice_fusion.8
  355.0 1.7 constant_dynamic-update-slice_fusion.7
  359.7 2.1 maximum_add_fusion.4
  364.4 2.5 maximum_add_fusion
  369.4 2.5 maximum_add_fusion.1
  378.4 1.9 copy.90
  380.2 1.9 copy.91
  382.1 1.9 copy.92
  384.0 1.9 constant_dynamic-update-slice_fusion.2
  385.9 1.7 constant_dynamic-update-slice_fusion.1
  387.6 1.7 constant_dynamic-update-slice_fusion
  389.3 89.7 %collective-permute-done.31 = f32[160,640]{1,0:T(8,128)} collective-permute-done((f32[160,640]{1,0:T(8,128)}, f32[160,640]{1,0:T(8,128)}, u32[]{:S(2)}, u32[]{:S(2)}) %collective-permute-start.31) | collective-permute-done | bytes 409632 | tf_op jit(solution)/shard_map/ppermute | solution.py:133
  479.0 1.9 fusion.71
  480.9 2.5 fusion.66
  483.4 2.8 fusion.60
  486.2 2.9 copy.98
  489.1 2.8 fusion.59
  (349 shorter events, 73.1 us)
Async XLA Ops:
  2.0 21.7 %collective-permute-start.5 = (f32[1,480]{1,0:T(1,128)}, f32[1,480]{1,0:T(1,128)S(1)}, u32[]{:S(2)}, u32[]{:S(2)}) collective-permute-start(f32[1,480]{1,0:T(1,128)} %reshape.240), channel_id=1, source_target_pairs={{0,2},{1,3},{2,0},{3,1},{4,6},{5,7},{6,4},{7,5}} | collective-permute-start | bytes 5768 | tf_op jit(solution)/shard_map/ppermute | solution.py:133
  5.3 41.6 %collective-permute-start.3 = (bf16[480,640]{1,0:T(8,128)(2,1)}, bf16[480,640]{1,0:T(8,128)(2,1)}, u32[]{:S(2)}, u32[]{:S(2)}) collective-permute-start(bf16[480,640]{1,0:T(8,128)(2,1)} %bitcast.200), channel_id=1, source_target_pairs={{0,2},{1,3},{2,0},{3,1},{4,6},{5,7},{6,4},{7,5}} | collective-permute-start | bytes 1843208 | tf_op jit(solution)/shard_map/ppermute | solution.py:133
  9.0 32.1 %collective-permute-start = (bf16[256,640]{0,1:T(8,128)(2,1)}, bf16[256,640]{0,1:T(8,128)(2,1)}, u32[]{:S(2)}, u32[]{:S(2)}) collective-permute-start(bf16[256,640]{0,1:T(8,128)(2,1)} %bitcast.1), channel_id=1, source_target_pairs={{0,1},{1,0},{2,3},{3,2},{4,5},{5,4},{6,7},{7,6}} | collective-permute-start | bytes 983048 | tf_op jit(solution)/shard_map/ppermute | solution.py:133
  9.9 33.4 %collective-permute-start.1 = (bf16[256,640]{0,1:T(8,128)(2,1)}, bf16[256,640]{0,1:T(8,128)(2,1)}, u32[]{:S(2)}, u32[]{:S(2)}) collective-permute-start(bf16[256,640]{0,1:T(8,128)(2,1)} %bitcast.2), channel_id=1, source_target_pairs={{0,2},{1,3},{2,0},{3,1},{4,6},{5,7},{6,4},{7,5}} | collective-permute-start | bytes 983048 | tf_op jit(solution)/shard_map/ppermute | solution.py:133
  11.9 16.9 %collective-permute-start.11 = (f32[640]{0:T(1024)S(1)}, f32[640]{0:T(1024)S(1)}, u32[]{:S(2)}, u32[]{:S(2)}) collective-permute-start(f32[640]{0:T(1024)S(1)} %copy-done.73), channel_id=1, source_target_pairs={{0,2},{1,3},{2,0},{3,1},{4,6},{5,7},{6,4},{7,5}} | collective-permute-start | bytes 7688 | tf_op jit(solution)/shard_map/ppermute | solution.py:133
  23.7 20.7 %collective-permute-start.2 = (bf16[256,640]{0,1:T(8,128)(2,1)}, bf16[256,640]{0,1:T(8,128)(2,1)}, u32[]{:S(2)}, u32[]{:S(2)}) collective-permute-start(bf16[256,640]{0,1:T(8,128)(2,1)} %bitcast.227), channel_id=1, source_target_pairs={{0,3},{1,2},{2,1},{3,0},{4,7},{5,6},{6,5},{7,4}} | collective-permute-start | bytes 983048 | tf_op jit(solution)/shard_map/ppermute | solution.py:133
  28.9 1.2 collective-permute-start.6
  30.0 1.2 collective-permute-start.12
  31.2 8.0 %collective-permute-start.7 = (bf16[160,640]{1,0:T(8,128)(2,1)}, bf16[160,640]{1,0:T(8,128)(2,1)S(1)}, u32[]{:S(2)}, u32[]{:S(2)}) collective-permute-start(bf16[160,640]{1,0:T(8,128)(2,1)} %bitcast.207), channel_id=1, source_target_pairs={{0,2},{1,3},{2,0},{3,1},{4,6},{5,7},{6,4},{7,5}} | collective-permute-start | bytes 614408 | tf_op jit(solution)/shard_map/ppermute | solution.py:133
  39.2 51.3 %collective-permute-start.9 = (bf16[640,640]{0,1:T(8,128)(2,1)S(1)}, bf16[640,640]{0,1:T(8,128)(2,1)S(1)}, u32[]{:S(2)}, u32[]{:S(2)}) collective-permute-start(bf16[640,640]{0,1:T(8,128)(2,1)S(1)} %copy.68), channel_id=1, source_target_pairs={{0,2},{1,3},{2,0},{3,1},{4,6},{5,7},{6,4},{7,5}} | collective-permute-start | bytes 2457608 | tf_op jit(solution)/shard_map/ppermute | solution.py:133
  40.1 7.9 %copy-start.29 = (bf16[3,640,5,32]{1,3,2,0:T(8,128)(2,1)S(1)}, bf16[3,640,5,32]{1,3,2,0:T(8,128)(2,1)}, u32[]{:S(2)}) copy-start(bf16[3,640,5,32]{1,3,2,0:T(8,128)(2,1)} %param.20) | copy-start | bytes 1843204
  41.2 51.5 %collective-permute-start.13 = (bf16[640,640]{1,0:T(8,128)(2,1)}, bf16[640,640]{1,0:T(8,128)(2,1)S(1)}, u32[]{:S(2)}, u32[]{:S(2)}) collective-permute-start(bf16[640,640]{1,0:T(8,128)(2,1)} %param.28), channel_id=1, source_target_pairs={{0,2},{1,3},{2,0},{3,1},{4,6},{5,7},{6,4},{7,5}} | collective-permute-start | bytes 2457608 | tf_op jit(solution)/shard_map/ppermute | solution.py:133
  43.3 5.9 %collective-permute-start.18 = (bf16[256,640]{0,1:T(8,128)(2,1)}, bf16[256,640]{0,1:T(8,128)(2,1)S(1)}, u32[]{:S(2)}, u32[]{:S(2)}) collective-permute-start(bf16[256,640]{0,1:T(8,128)(2,1)} %bitcast.226), channel_id=1, source_target_pairs={{0,1},{1,0},{2,3},{3,2},{4,5},{5,4},{6,7},{7,6}} | collective-permute-start | bytes 983048 | tf_op jit(solution)/shard_map/ppermute | solution.py:133
  44.4 40.5 %collective-permute-start.19 = (bf16[256,640]{0,1:T(8,128)(2,1)}, bf16[256,640]{0,1:T(8,128)(2,1)S(1)}, u32[]{:S(2)}, u32[]{:S(2)}) collective-permute-start(bf16[256,640]{0,1:T(8,128)(2,1)} %bitcast.225), channel_id=1, source_target_pairs={{0,2},{1,3},{2,0},{3,1},{4,6},{5,7},{6,4},{7,5}} | collective-permute-start | bytes 983048 | tf_op jit(solution)/shard_map/ppermute | solution.py:133
  46.3 47.9 %copy-start.5 = (bf16[1024,640]{0,1:T(8,128)(2,1)}, bf16[1024,640]{0,1:T(8,128)(2,1)S(1)}, u32[]{:S(2)}) copy-start(bf16[1024,640]{0,1:T(8,128)(2,1)S(1)} %constant_dynamic-update-slice_fusion.9) | copy-start | bytes 3932164
  46.6 47.7 %copy-start.66 = (f32[1024]{0:T(1024)}, f32[1024]{0:T(1024)S(1)}, u32[]{:S(2)}) copy-start(f32[1024]{0:T(1024)S(1)} %broadcast_multiply_fusion.8) | copy-start | bytes 12292
  47.0 42.3 %collective-permute-start.20 = (bf16[256,640]{0,1:T(8,128)(2,1)S(1)}, bf16[256,640]{0,1:T(8,128)(2,1)S(1)}, u32[]{:S(2)}, u32[]{:S(2)}) collective-permute-start(bf16[256,640]{0,1:T(8,128)(2,1)S(1)} %bitcast.224), channel_id=1, source_target_pairs={{0,3},{1,2},{2,1},{3,0},{4,7},{5,6},{6,5},{7,4}} | collective-permute-start | bytes 983048 | tf_op jit(solution)/shard_map/ppermute | solution.py:133
  48.0 41.5 %copy-start.46 = (bf16[5,32,640]{2,1,0:T(8,128)(2,1)S(1)}, bf16[5,32,640]{2,1,0:T(8,128)(2,1)}, u32[]{:S(2)}) copy-start(bf16[5,32,640]{2,1,0:T(8,128)(2,1)} %param.22) | copy-start | bytes 614404
  49.2 44.9 %collective-permute-start.4 = (bf16[2,480,640]{2,1,0:T(8,128)(2,1)S(1)}, bf16[2,480,640]{2,1,0:T(8,128)(2,1)S(1)}, u32[]{:S(2)}, u32[]{:S(2)}) collective-permute-start(bf16[2,480,640]{2,1,0:T(8,128)(2,1)S(1)} %pad_maximum_fusion.9), channel_id=1, source_target_pairs={{0,1},{1,0},{2,3},{3,2},{4,5},{5,4},{6,7},{7,6}} | collective-permute-start | bytes 3686408 | tf_op jit(solution)/shard_map/ppermute | solution.py:133
  84.9 4.5 collective-permute-start.8
  91.9 52.0 %collective-permute-start.10 = (bf16[2,640,640]{1,2,0:T(8,128)(2,1)}, bf16[2,640,640]{1,2,0:T(8,128)(2,1)}, u32[]{:S(2)}, u32[]{:S(2)}) collective-permute-start(bf16[2,640,640]{1,2,0:T(8,128)(2,1)} %pad_maximum_fusion.7), channel_id=1, source_target_pairs={{0,1},{1,0},{2,3},{3,2},{4,5},{5,4},{6,7},{7,6}} | collective-permute-start | bytes 4915208 | tf_op jit(solution)/shard_map/ppermute | solution.py:133
  94.1 59.9 %collective-permute-start.14 = (bf16[2,640,640]{2,1,0:T(8,128)(2,1)}, bf16[2,640,640]{2,1,0:T(8,128)(2,1)}, u32[]{:S(2)}, u32[]{:S(2)}) collective-permute-start(bf16[2,640,640]{2,1,0:T(8,128)(2,1)} %pad_maximum_fusion.8), channel_id=1, source_target_pairs={{0,1},{1,0},{2,3},{3,2},{4,5},{5,4},{6,7},{7,6}} | collective-permute-start | bytes 4915208 | tf_op jit(solution)/shard_map/ppermute | solution.py:133
  104.0 34.4 %copy-start.30 = (bf16[3,640,5,32]{1,3,2,0:T(8,128)(2,1)S(1)}, bf16[3,640,5,32]{1,3,2,0:T(8,128)(2,1)}, u32[]{:S(2)}) copy-start(bf16[3,640,5,32]{1,3,2,0:T(8,128)(2,1)} %param.20) | copy-start | bytes 1843204
  104.0 34.4 %copy-start.32 = (bf16[1,480,640]{2,1,0:T(8,128)(2,1)S(1)}, bf16[1,480,640]{2,1,0:T(8,128)(2,1)}, u32[]{:S(2)}) copy-start(bf16[1,480,640]{2,1,0:T(8,128)(2,1)} %copy-done.31) | copy-start | bytes 1843204
  104.0 34.4 %copy-start.34 = (bf16[1,480,640]{2,1,0:T(8,128)(2,1)S(1)}, bf16[1,480,640]{2,1,0:T(8,128)(2,1)}, u32[]{:S(2)}) copy-start(bf16[1,480,640]{2,1,0:T(8,128)(2,1)} %copy-done.33) | copy-start | bytes 1843204
  143.4 10.5 %copy-start.13 = (bf16[1024,640]{0,1:T(8,128)(2,1)}, bf16[1024,640]{0,1:T(8,128)(2,1)S(1)}, u32[]{:S(2)}) copy-start(bf16[1024,640]{0,1:T(8,128)(2,1)S(1)} %get-tuple-element.149) | copy-start | bytes 3932164
  155.6 9.2 %copy-start.57 = (bf16[1,640,640]{2,1,0:T(8,128)(2,1)}, bf16[1,640,640]{2,1,0:T(8,128)(2,1)S(1)}, u32[]{:S(2)}) copy-start(bf16[1,640,640]{2,1,0:T(8,128)(2,1)S(1)} %get-tuple-element.100) | copy-start | bytes 2457604
  155.7 9.2 %copy-start.59 = (bf16[1,640,640]{2,1,0:T(8,128)(2,1)}, bf16[1,640,640]{2,1,0:T(8,128)(2,1)S(1)}, u32[]{:S(2)}) copy-start(bf16[1,640,640]{2,1,0:T(8,128)(2,1)S(1)} %get-tuple-element.101) | copy-start | bytes 2457604
  180.4 67.4 %copy-start.8 = (f32[1024,640]{0,1:T(8,128)}, f32[1024,640]{0,1:T(8,128)S(1)}, u32[]{:S(2)}) copy-start(f32[1024,640]{0,1:T(8,128)S(1)} %get-tuple-element.71) | copy-start | bytes 7864324
  182.7 56.2 %copy-start.45 = (f32[32,1024]{1,0:T(8,128)S(1)}, f32[32,1024]{1,0:T(8,128)}, u32[]{:S(2)}) copy-start(f32[32,1024]{1,0:T(8,128)} %get-tuple-element.133) | copy-start | bytes 393220
  248.4 11.2 %slice-start.2 = ((s8[5242880]{0:T(1024)(128)(4,1)}), s8[4194304]{0:T(1024)(128)(4,1)S(1)}, s32[]{:S(2)}) async-start(s8[5242880]{0:T(1024)(128)(4,1)} %bitcast.234), calls=%async_computation.2 | async-start | bytes 8388608
  249.7 9.9 %copy-start.24 = (bf16[1024,640]{0,1:T(8,128)(2,1)S(1)}, bf16[1024,640]{0,1:T(8,128)(2,1)}, u32[]{:S(2)}) copy-start(bf16[1024,640]{0,1:T(8,128)(2,1)} %copy-done.22) | copy-start | bytes 3932164
  249.7 9.9 %slice-start.3 = ((s8[5242880]{0:T(1024)(128)(4,1)}), s8[1048576]{0:T(1024)(128)(4,1)S(1)}, s32[]{:S(2)}) async-start(s8[5242880]{0:T(1024)(128)(4,1)} %bitcast.234), calls=%async_computation.3 | async-start | bytes 2097152
  272.1 7.8 %copy-start.26 = (bf16[4,3,5,32,1024]{4,3,2,1,0:T(8,128)(2,1)S(1)}, bf16[4,3,5,32,1024]{4,3,2,1,0:T(8,128)(2,1)}, u32[]{:S(2)}) copy-start(bf16[4,3,5,32,1024]{4,3,2,1,0:T(8,128)(2,1)} %fusion.10) | copy-start | bytes 11796484
  272.2 7.8 %copy-start.28 = (bf16[4,480,640]{2,1,0:T(8,128)(2,1)S(1)}, bf16[4,480,640]{2,1,0:T(8,128)(2,1)}, u32[]{:S(2)}) copy-start(bf16[4,480,640]{2,1,0:T(8,128)(2,1)} %pad_maximum_fusion.5) | copy-start | bytes 7372804
  295.9 23.0 %collective-permute-start.24 = (f32[2,640]{1,0:T(2,128)S(1)}, f32[2,640]{1,0:T(2,128)S(1)}, u32[]{:S(2)}, u32[]{:S(2)}) collective-permute-start(f32[2,640]{1,0:T(2,128)S(1)} %pad_maximum_fusion.21), channel_id=1, source_target_pairs={{0,1},{1,0},{2,3},{3,2},{4,5},{5,4},{6,7},{7,6}} | collective-permute-start | bytes 15368 | tf_op jit(solution)/shard_map/ppermute | solution.py:133
  301.3 57.1 %collective-permute-start.26 = (f32[2,480,640]{2,1,0:T(8,128)}, f32[2,480,640]{2,1,0:T(8,128)}, u32[]{:S(2)}, u32[]{:S(2)}) collective-permute-start(f32[2,480,640]{2,1,0:T(8,128)} %pad_maximum_fusion.6), channel_id=1, source_target_pairs={{0,1},{1,0},{2,3},{3,2},{4,5},{5,4},{6,7},{7,6}} | collective-permute-start | bytes 7372808 | tf_op jit(solution)/shard_map/ppermute | solution.py:133
  302.0 16.3 %collective-permute-start.28 = (f32[2,480]{1,0:T(2,128)S(1)}, f32[2,480]{1,0:T(2,128)S(1)}, u32[]{:S(2)}, u32[]{:S(2)}) collective-permute-start(f32[2,480]{1,0:T(2,128)S(1)} %pad_maximum_fusion.24), channel_id=1, source_target_pairs={{0,1},{1,0},{2,3},{3,2},{4,5},{5,4},{6,7},{7,6}} | collective-permute-start | bytes 11528 | tf_op jit(solution)/shard_map/ppermute | solution.py:133
  310.2 52.6 %collective-permute-start.34 = (f32[2,640,640]{1,2,0:T(8,128)}, f32[2,640,640]{1,2,0:T(8,128)}, u32[]{:S(2)}, u32[]{:S(2)}) collective-permute-start(f32[2,640,640]{1,2,0:T(8,128)} %pad_maximum_fusion.3), channel_id=1, source_target_pairs={{0,1},{1,0},{2,3},{3,2},{4,5},{5,4},{6,7},{7,6}} | collective-permute-start | bytes 9830408 | tf_op jit(solution)/shard_map/ppermute | solution.py:133
  310.7 8.1 %collective-permute-start.36 = (f32[2,640]{1,0:T(2,128)S(1)}, f32[2,640]{1,0:T(2,128)S(1)}, u32[]{:S(2)}, u32[]{:S(2)}) collective-permute-start(f32[2,640]{1,0:T(2,128)S(1)} %pad_maximum_fusion.22), channel_id=1, source_target_pairs={{0,1},{1,0},{2,3},{3,2},{4,5},{5,4},{6,7},{7,6}} | collective-permute-start | bytes 15368 | tf_op jit(solution)/shard_map/ppermute | solution.py:133
  316.1 13.6 %copy-start.36 = (f32[1,160,640]{2,1,0:T(8,128)S(1)}, f32[1,160,640]{2,1,0:T(8,128)}, u32[]{:S(2)}) copy-start(f32[1,160,640]{2,1,0:T(8,128)} %get-tuple-element.97) | copy-start | bytes 1228804
  316.1 13.6 %copy-start.37 = (f32[1,160,640]{2,1,0:T(8,128)S(1)}, f32[1,160,640]{2,1,0:T(8,128)}, u32[]{:S(2)}) copy-start(f32[1,160,640]{2,1,0:T(8,128)} %get-tuple-element.98) | copy-start | bytes 1228804
  316.1 17.2 %copy-start.62 = (bf16[256,640]{0,1:T(8,128)(2,1)S(1)}, bf16[256,640]{0,1:T(8,128)(2,1)}, u32[]{:S(2)}) copy-start(bf16[256,640]{0,1:T(8,128)(2,1)} %get-tuple-element.114) | copy-start | bytes 983044
  318.2 39.0 %copy-start.35 = (f32[1,160,640]{2,1,0:T(8,128)S(1)}, f32[1,160,640]{2,1,0:T(8,128)}, u32[]{:S(2)}) copy-start(f32[1,160,640]{2,1,0:T(8,128)} %get-tuple-element.99) | copy-start | bytes 1228804
  318.3 49.8 %collective-permute-start.38 = (f32[2,640,640]{2,1,0:T(8,128)}, f32[2,640,640]{2,1,0:T(8,128)}, u32[]{:S(2)}, u32[]{:S(2)}) collective-permute-start(f32[2,640,640]{2,1,0:T(8,128)} %pad_maximum_fusion.4), channel_id=1, source_target_pairs={{0,1},{1,0},{2,3},{3,2},{4,5},{5,4},{6,7},{7,6}} | collective-permute-start | bytes 9830408 | tf_op jit(solution)/shard_map/ppermute | solution.py:133
  318.8 3.6 collective-permute-start.29
  318.9 7.1 %collective-permute-start.32 = (f32[4,640]{1,0:T(4,128)S(1)}, f32[4,640]{1,0:T(4,128)S(1)}, u32[]{:S(2)}, u32[]{:S(2)}) collective-permute-start(f32[4,640]{1,0:T(4,128)S(1)} %pad_maximum_fusion.19), channel_id=1, source_target_pairs={{0,1},{1,0},{2,3},{3,2},{4,5},{5,4},{6,7},{7,6}} | collective-permute-start | bytes 30728 | tf_op jit(solution)/shard_map/ppermute | solution.py:133
  322.5 3.6 collective-permute-start.37
  326.1 7.9 %collective-permute-start.15 = (bf16[256,640]{0,1:T(8,128)(2,1)}, bf16[256,640]{0,1:T(8,128)(2,1)}, u32[]{:S(2)}, u32[]{:S(2)}) collective-permute-start(bf16[256,640]{0,1:T(8,128)(2,1)} %get-tuple-element.115), channel_id=1, source_target_pairs={{0,1},{1,0},{2,3},{3,2},{4,5},{5,4},{6,7},{7,6}} | collective-permute-start | bytes 983048 | tf_op jit(solution)/shard_map/ppermute | solution.py:133
  326.1 3.6 collective-permute-start.25
  329.7 3.7 collective-permute-start.33
  333.4 7.8 %collective-permute-start.16 = (bf16[256,640]{0,1:T(8,128)(2,1)S(1)}, bf16[256,640]{0,1:T(8,128)(2,1)S(1)}, u32[]{:S(2)}, u32[]{:S(2)}) collective-permute-start(bf16[256,640]{0,1:T(8,128)(2,1)S(1)} %copy-done.62), channel_id=1, source_target_pairs={{0,2},{1,3},{2,0},{3,1},{4,6},{5,7},{6,4},{7,5}} | collective-permute-start | bytes 983048 | tf_op jit(solution)/shard_map/ppermute | solution.py:133
  334.0 22.8 %collective-permute-start.30 = (f32[2,160,640]{2,1,0:T(8,128)}, f32[2,160,640]{2,1,0:T(8,128)}, u32[]{:S(2)}, u32[]{:S(2)}) collective-permute-start(f32[2,160,640]{2,1,0:T(8,128)} %pad_maximum_fusion.11), channel_id=1, source_target_pairs={{0,1},{1,0},{2,3},{3,2},{4,5},{5,4},{6,7},{7,6}} | collective-permute-start | bytes 2457608 | tf_op jit(solution)/shard_map/ppermute | solution.py:133
  341.2 10.0 %collective-permute-start.17 = (bf16[256,640]{0,1:T(8,128)(2,1)}, bf16[256,640]{0,1:T(8,128)(2,1)}, u32[]{:S(2)}, u32[]{:S(2)}) collective-permute-start(bf16[256,640]{0,1:T(8,128)(2,1)} %get-tuple-element.113), channel_id=1, source_target_pairs={{0,3},{1,2},{2,1},{3,0},{4,7},{5,6},{6,5},{7,4}} | collective-permute-start | bytes 983048 | tf_op jit(solution)/shard_map/ppermute | solution.py:133
  343.8 15.8 %copy-start.25 = (f32[1,480,640]{2,1,0:T(8,128)S(1)}, f32[1,480,640]{2,1,0:T(8,128)}, u32[]{:S(2)}) copy-start(f32[1,480,640]{2,1,0:T(8,128)} %get-tuple-element.87) | copy-start | bytes 3686404
  351.2 23.6 %collective-permute-start.21 = (bf16[256,640]{0,1:T(8,128)(2,1)}, bf16[256,640]{0,1:T(8,128)(2,1)}, u32[]{:S(2)}, u32[]{:S(2)}) collective-permute-start(bf16[256,640]{0,1:T(8,128)(2,1)} %get-tuple-element.107), channel_id=1, source_target_pairs={{0,1},{1,0},{2,3},{3,2},{4,5},{5,4},{6,7},{7,6}} | collective-permute-start | bytes 983048 | tf_op jit(solution)/shard_map/ppermute | solution.py:133
  356.7 19.6 %collective-permute-start.22 = (bf16[256,640]{0,1:T(8,128)(2,1)}, bf16[256,640]{0,1:T(8,128)(2,1)S(1)}, u32[]{:S(2)}, u32[]{:S(2)}) collective-permute-start(bf16[256,640]{0,1:T(8,128)(2,1)} %get-tuple-element.106), channel_id=1, source_target_pairs={{0,2},{1,3},{2,0},{3,1},{4,6},{5,7},{6,4},{7,5}} | collective-permute-start | bytes 983048 | tf_op jit(solution)/shard_map/ppermute | solution.py:133
  358.4 17.2 %copy-start.27 = (f32[2,160,640]{2,1,0:T(8,128)}, f32[2,160,640]{2,1,0:T(8,128)S(1)}, u32[]{:S(2)}) copy-start(f32[2,160,640]{2,1,0:T(8,128)S(1)} %maximum_add_fusion.5) | copy-start | bytes 2457604
  358.4 23.7 %collective-permute-start.23 = (bf16[256,640]{0,1:T(8,128)(2,1)}, bf16[256,640]{0,1:T(8,128)(2,1)}, u32[]{:S(2)}, u32[]{:S(2)}) collective-permute-start(bf16[256,640]{0,1:T(8,128)(2,1)} %get-tuple-element.105), channel_id=1, source_target_pairs={{0,3},{1,2},{2,1},{3,0},{4,7},{5,6},{6,5},{7,4}} | collective-permute-start | bytes 983048 | tf_op jit(solution)/shard_map/ppermute | solution.py:133
  362.9 118.1 %collective-permute-start.27 = (f32[480,640]{1,0:T(8,128)}, f32[480,640]{1,0:T(8,128)}, u32[]{:S(2)}, u32[]{:S(2)}) collective-permute-start(f32[480,640]{1,0:T(8,128)} %slice_bitcast_fusion.4), channel_id=1, source_target_pairs={{0,2},{1,3},{2,0},{3,1},{4,6},{5,7},{6,4},{7,5}} | collective-permute-start | bytes 3686408 | tf_op jit(solution)/shard_map/ppermute | solution.py:133
  368.1 115.3 %collective-permute-start.35 = (f32[640,640]{0,1:T(8,128)}, f32[640,640]{0,1:T(8,128)}, u32[]{:S(2)}, u32[]{:S(2)}) collective-permute-start(f32[640,640]{0,1:T(8,128)} %slice_bitcast_fusion.2), channel_id=1, source_target_pairs={{0,2},{1,3},{2,0},{3,1},{4,6},{5,7},{6,4},{7,5}} | collective-permute-start | bytes 4915208 | tf_op jit(solution)/shard_map/ppermute | solution.py:133
  374.8 114.3 %collective-permute-start.39 = (f32[640,640]{1,0:T(8,128)}, f32[640,640]{1,0:T(8,128)}, u32[]{:S(2)}, u32[]{:S(2)}) collective-permute-start(f32[640,640]{1,0:T(8,128)} %slice_bitcast_fusion), channel_id=1, source_target_pairs={{0,2},{1,3},{2,0},{3,1},{4,6},{5,7},{6,4},{7,5}} | collective-permute-start | bytes 4915208 | tf_op jit(solution)/shard_map/ppermute | solution.py:133
  376.4 102.6 %collective-permute-start.31 = (f32[160,640]{1,0:T(8,128)}, f32[160,640]{1,0:T(8,128)}, u32[]{:S(2)}, u32[]{:S(2)}) collective-permute-start(f32[160,640]{1,0:T(8,128)} %slice_bitcast_fusion.10), channel_id=1, source_target_pairs={{0,2},{1,3},{2,0},{3,1},{4,6},{5,7},{6,4},{7,5}} | collective-permute-start | bytes 1228808 | tf_op jit(solution)/shard_map/ppermute | solution.py:133
  384.0 96.9 %copy-start.17 = (f32[2,480,640]{2,1,0:T(8,128)S(1)}, f32[2,480,640]{2,1,0:T(8,128)}, u32[]{:S(2)}) copy-start(f32[2,480,640]{2,1,0:T(8,128)} %copy-done.16) | copy-start | bytes 7372804
  (60 other events, 196.3 us)

commit v2 on v0

v2 whole, which is shorter than its diff:
```python
import functools

import jax
import jax.numpy as jnp
import numpy as np
from jax import lax
from jax.experimental import pallas as pl
from jax.experimental.pallas import tpu as pltpu
from jax.sharding import PartitionSpec as P

LN_EPS = 1e-5
ROPE_BASE = 10000.0
INV_SQRT2 = 0.7071067811865476
INV_SQRT_2PI = 0.3989422804014327
NEG_LARGE = -1e30
F32 = jnp.float32
BF16 = jnp.bfloat16
MESH = pl.DeviceIdType.MESH


def dot(lhs, rhs):
    return jnp.dot(lhs, rhs, preferred_element_type=F32)


def layer_norm(values, ln_gain, ln_bias):
    centered = values - jnp.mean(values, axis=-1, keepdims=True)
    inv_std = lax.rsqrt(jnp.mean(centered * centered, axis=-1, keepdims=True) + LN_EPS)
    x_hat = centered * inv_std
    return x_hat * ln_gain + ln_bias, x_hat, inv_std


def rope_tables(seq_len, head_dim):
    half_dim = head_dim // 2
    inv_freq = np.float32(ROPE_BASE) ** (np.float32(-2.0) * np.arange(half_dim, dtype=np.float32) / np.float32(head_dim))
    angles = inv_freq[:, None] * np.arange(seq_len, dtype=np.float32)[None, :]
    return np.cos(angles), np.sin(angles)


def remote(src, dst, send_sem, recv_sem, device):
    return pltpu.make_async_remote_copy(src_ref=src, dst_ref=dst, send_sem=send_sem, recv_sem=recv_sem, device_id={'tp': device}, device_id_type=MESH)


def greet(me, groups=False):
    barrier = pltpu.get_barrier_semaphore()
    for mask in (1, 2, 3):
        pl.semaphore_signal(barrier, inc=1, device_id={'tp': me ^ mask}, device_id_type=MESH)
    if groups:
        pl.semaphore_signal(barrier, inc=1, device_id={'dp': lax.axis_index('dp') ^ 1}, device_id_type=MESH)
    pl.semaphore_wait(barrier, 4 if groups else 3)


class Gather:
    def __init__(self, src, dst, base, send_sem, recv_sem, me):
        self.near = remote(src, dst.at[1 - base], send_sem.at[0], recv_sem.at[0], me ^ 1)
        self.far = remote(src, dst.at[2 - base], send_sem.at[1], recv_sem.at[1], me ^ 2)
        self.relay = remote(dst.at[2 - base], dst.at[3 - base], send_sem.at[2], recv_sem.at[2], me ^ 1)

    def start(self):
        self.far.start()
        self.near.start()

    def forward(self):
        self.far.wait_recv()
        self.relay.start()

    def finish(self):
        self.near.wait()
        self.far.wait_send()
        self.relay.wait()


class SharedGather:
    def __init__(self, src, dst, send_sem, recv_sem, me):
        group = lax.axis_index('dp')
        half, rest = group, group ^ 1
        self.near = remote(src, dst.at[1], send_sem.at[0], recv_sem.at[0], me ^ 1)
        self.far = remote(src.at[half], dst.at[2, half], send_sem.at[1], recv_sem.at[1], me ^ 2)
        self.side = pltpu.make_async_remote_copy(src_ref=dst.at[2, half], dst_ref=dst.at[2, half], send_sem=send_sem.at[2], recv_sem=recv_sem.at[2], device_id={'dp': rest}, device_id_type=MESH)
        self.relay = Copies([remote(dst.at[2, part], dst.at[3, part], send_sem.at[3 + i], recv_sem.at[3 + i], me ^ 1) for i, part in enumerate((half, rest))])

    def start(self):
        self.far.start()
        self.near.start()

    def forward(self):
        self.far.wait_recv()
        self.side.start()
        self.relay.copies[0].start()

    def forward_rest(self):
        self.side.wait_recv()
        self.relay.copies[1].start()

    def wait_send(self):
        for copy in (self.near, self.far, self.side, self.relay):
            copy.wait_send()


def layer_norm_rows(values, ln_gain, ln_bias):
    centered = values - jnp.mean(values, axis=0, keepdims=True)
    inv_std = lax.rsqrt(jnp.mean(centered * centered, axis=0, keepdims=True) + LN_EPS)
    x_hat = centered * inv_std
    return x_hat * ln_gain + ln_bias, x_hat, inv_std


def layer_norm_rows_grad(d_out, x_hat, inv_std, ln_gain):
    d_hat = d_out * ln_gain
    return inv_std * (d_hat - jnp.mean(d_hat, axis=0, keepdims=True) - x_hat * jnp.mean(d_hat * x_hat, axis=0, keepdims=True))


def dot_tn(lhs, rhs):
    return lax.dot_general(lhs, rhs, (((0,), (0,)), ((), ())), preferred_element_type=F32)


def dot_nt(lhs, rhs):
    return lax.dot_general(lhs, rhs, (((1,), (1,)), ((), ())), preferred_element_type=F32)


def gelu(pre_act):
    half_erf = 0.5 * (1.0 + lax.erf(pre_act * INV_SQRT2))
    act = (pre_act * half_erf).astype(BF16)
    return act, half_erf + pre_act * jnp.exp(-0.5 * pre_act * pre_act) * INV_SQRT_2PI


class Copies:
    def __init__(self, copies):
        self.copies = copies

    def start(self):
        for copy in self.copies:
            copy.start()

    def wait(self):
        for copy in self.copies:
            copy.wait()

    def wait_recv(self):
        for copy in self.copies:
            copy.wait_recv()

    def wait_send(self):
        for copy in self.copies:
            copy.wait_send()


def rows_of(owner, chunk):
    return pl.ds(pl.multiple_of(owner * chunk, chunk), chunk)


def to_sequence(src, dst, send_sem, recv_sem, me, chunk):
    return Copies([remote(src.at[me ^ mask], dst.at[rows_of(me, chunk)], send_sem.at[mask], recv_sem.at[mask], me ^ mask) for mask in (2, 3, 1)])


def from_sequence(src, dst, send_sem, recv_sem, me, chunk):
    return Copies([remote(src.at[rows_of(me ^ mask, chunk)], dst.at[me], send_sem.at[mask], recv_sem.at[mask], me ^ mask) for mask in (2, 3, 1)])


def lane_sum(value):
    return jnp.sum(value, axis=1, keepdims=True)


def forward_kernel(dims, x_ref, wq_ref, bq_ref, mask_ref, vec_ref, cos_ref, sin_ref, wo_ref, wu_ref, wd_ref, dy_ref,
                   x_out, wq_out, h1_out, q_out, k_out, v_out, o_out, wide_out, lse_out, y_out, h2_out, dx1t_out, dx1b_out, do_out, dy_out, h2_all, dy_cross, sums_ref,
                   x_full, wq_all, h1_ref, q_all, k_all, v_all, o_ref, wide_ref, lse_ref, h1t_ref, bq_all, wo_all, wu_all, wd_all, vec_all, dy_full,
                   act_ref, stage_ref, wide_stage, own_sem, once_sem, store_sem, x_send, x_recv, dy_send, dy_recv, send_sem, recv_sem, wide_send, wide_recv):
    chunk, local_heads, head_dim = dims
    me = lax.axis_index('tp')
    half = head_dim // 2
    seq_len, width = x_full.shape
    tp, ff = wu_all.shape[0], wu_ref.shape[2]
    greet(me, True)
    x_move = to_sequence(x_ref, x_full, x_send, x_recv, me, chunk)
    dy_move = to_sequence(dy_ref, dy_full, dy_send, dy_recv, me, chunk)
    dy_far = Copies([remote(dy_ref.at[me ^ i], dy_cross.at[i], dy_send.at[4 + i], dy_recv.at[4 + i], me ^ 2) for i in (0, 1)])
    gathered = ((bq_ref, bq_all), (vec_ref, vec_all))
    moves = [Gather(source, dst, 0, send_sem.at[i], recv_sem.at[i], me) for i, (source, dst) in enumerate(gathered)]
    bq, vec = moves
    weights = ((wq_ref, wq_all), (wo_ref, wo_all), (wu_ref, wu_all), (wd_ref, wd_all))
    shared = [SharedGather(source, dst, wide_send.at[i], wide_recv.at[i], me) for i, (source, dst) in enumerate(weights)]
    wq, wo, wu, wd = shared
    own = [pltpu.make_async_copy(source, dst.at[0], own_sem.at[i]) for i, (source, dst) in enumerate(gathered + weights)]
    x_move.start()
    bq.start()
    wq.start()
    for copy in own:
        copy.start()
    for move in (vec, wo, wu, wd, dy_move, dy_far):
        move.start()
    own_rows = rows_of(me, chunk)
    own_x = pltpu.make_async_copy(x_ref.at[me], x_full.at[own_rows], once_sem.at[0])
    own_dy = pltpu.make_async_copy(dy_ref.at[me], dy_full.at[own_rows], once_sem.at[1])
    own_x.start()
    own_dy.start()
    valid = mask_ref[pl.ds(me, 1)] > 0
    first = lax.broadcasted_iota(jnp.int32, (half, seq_len), 0) == 0
    ones = first.astype(F32).astype(BF16)
    key_bias = jnp.where(first, jnp.where(valid, 0.0, NEG_LARGE), 0.0).astype(BF16)
    for copy in own:
        copy.wait()
    own_x.wait()
    x_move.wait_recv()
    h1, _, _ = layer_norm(x_full[...].astype(F32), vec_all[0, 4:5], vec_all[0, 5:6])
    h1 = h1.astype(BF16)
    h1_ref[...] = h1
    h1t_ref[...] = h1.T
    once = [pltpu.make_async_copy(source, dst, once_sem.at[2 + i]) for i, (source, dst) in enumerate((
        (x_full, x_out), (h1_ref, h1_out), (wq_all, wq_out), (stage_ref.at[0], h2_out), (stage_ref.at[1], y_out), (stage_ref.at[2], dx1b_out), (wide_stage, dx1t_out), (dy_full, dy_out)))]
    once[0].start()
    once[1].start()

    def stores(m):
        heads = pl.ds(m * local_heads, local_heads)
        pairs = ((q_all, q_out), (k_all, k_out), (v_all, v_out), (o_ref, o_out), (wide_ref, wide_out), (lse_ref, lse_out))
        return Copies([pltpu.make_async_copy(source.at[heads], dst.at[heads], store_sem.at[i, m]) for i, (source, dst) in enumerate(pairs)])

    @pl.loop(0, 4)
    def _(m):
        @pl.when(m == 1)
        def _():
            bq.near.wait_recv()
            wq.near.wait_recv()
            bq.forward()
            wq.forward()

        @pl.when(m == 2)
        def _():
            wq.forward_rest()
            vec.forward()
            wo.forward()

        @pl.when(m == 3)
        def _():
            bq.relay.wait_recv()
            wq.relay.wait_recv()
            once[2].start()
            wo.forward_rest()
            wu.forward()
            wd.forward()

        bias = bq_all[m].T[:, :1]
        qkv = dot(wq_all[m].reshape(bias.shape[0], width), h1t_ref[...]) + bias
        cos, sin = cos_ref[...], sin_ref[...]
        group = local_heads * head_dim
        for j in range(local_heads):
            head = m * local_heads + j
            for which, (dst, scale, extra) in enumerate(((q_all, head_dim ** -0.5, ones), (k_all, None, key_bias))):
                rows = qkv[which * group + j * head_dim:which * group + (j + 1) * head_dim]
                rows = rows * scale if scale is not None else rows
                low, high = rows[:half], rows[half:]
                dst[head, :half] = (low * cos - high * sin).astype(BF16)
                dst[head, half:head_dim] = (high * cos + low * sin).astype(BF16)
                dst[head, head_dim:] = extra
            v_all[head] = qkv[2 * group + j * head_dim:2 * group + (j + 1) * head_dim].astype(BF16)

        @pl.loop(0, local_heads)
        def _(j):
            head = m * local_heads + j
            scores = dot(k_all[head].T, q_all[head])
            top = jnp.max(scores, axis=0, keepdims=True)
            weights = jnp.exp(scores - top)
            total = jnp.sum(weights, axis=0, keepdims=True)
            out = dot(v_all[head], weights.astype(BF16)) / total
            o_ref[head] = out.astype(BF16)
            wide_ref[head] = out
            lse_ref[head] = top + jnp.log(total)

        stores(m).start()

    wu.forward_rest()
    wd.forward_rest()
    for move in (vec, wo):
        move.near.wait_recv()
        move.relay.wait_recv()
    rows = tp * local_heads * head_dim
    wo_full = wo_all[...].reshape(rows, width)
    cols = vec_all[0].T
    b_out, gain, bias, b_down = (cols[:, i:i + 1] for i in range(4))
    attn = dot_tn(wo_full, o_ref[...].reshape(rows, seq_len))
    x1 = (x_full[...].T.astype(F32) + (attn + b_out)).astype(BF16).astype(F32)
    h2_f, x_hat, inv_std = layer_norm_rows(x1, gain, bias)
    h2 = h2_f.astype(BF16)
    stage_ref[0] = h2.T
    wu.near.wait_recv()
    wu.relay.wait_recv()
    h2_move = Gather(stage_ref.at[0, :h2_all.shape[1]], h2_all, 1, send_sem.at[2], recv_sem.at[2], me)

    def mlp(slope_ref):
        @pl.loop(0, tp)
        def _(m):
            @pl.when(m == 1)
            def _():
                h2_move.start()
                once[3].start()

            pre_act = dot_tn(wu_all[m].reshape(width, ff), h2) + vec_all[m].T[:, 6:7]
            act, slope = gelu(pre_act)
            act_ref[m] = act
            slope_ref[m] = slope

        wd.near.wait_recv()
        wd.relay.wait_recv()
        out = dot_tn(wd_all[...].reshape(tp * ff, width), act_ref[...].reshape(tp * ff, seq_len))
        stage_ref[1] = (x1 + (out + b_down)).astype(BF16).T
        own_dy.wait()
        dy_move.wait_recv()
        once[7].start()
        dy_t = dy_full[...].T

        @pl.loop(0, tp)
        def _(m):
            @pl.when(m == 1)
            def _():
                once[4].start()

            act_ref[m] = (dot(wd_all[m].reshape(ff, width), dy_t) * slope_ref[m]).astype(BF16)

    pl.run_scoped(mlp, pltpu.VMEM((tp, ff, seq_len), F32))
    d_h2 = dot(wu_all[0].reshape(width, ff), act_ref[0])
    for m in range(1, tp):
        d_h2 = d_h2 + dot(wu_all[m].reshape(width, ff), act_ref[m])
    dy_f = dy_full[...].T.astype(F32)
    d_x1 = dy_f + layer_norm_rows_grad(d_h2, x_hat, inv_std, gain)
    d_x1_b = d_x1.astype(BF16)
    wide_stage[...] = d_x1
    stage_ref[2] = d_x1_b.T
    for m in range(4):
        stores(m).wait()
    o_ref[...] = dot(wo_full, d_x1_b).astype(BF16).reshape(o_ref.shape)
    h2_move.forward()
    once[5].start()
    once[6].start()
    sums = [lane_sum(dy_f), lane_sum(d_h2 * x_hat), lane_sum(d_h2), lane_sum(d_x1)]
    sums_ref[...] = jnp.concatenate(sums + [jnp.zeros((width, 124), F32)], axis=1).T[:8]
    last = pltpu.make_async_copy(o_ref, do_out, once_sem.at[10])
    last.start()
    x_move.wait_send()
    dy_move.wait_send()
    dy_far.wait()
    for move in moves:
        move.near.wait_send()
        move.far.wait_send()
        move.relay.wait_send()
    for move in shared:
        move.wait_send()
    for copy in once:
        copy.wait()
    last.wait()
    h2_move.finish()


def backward_kernel(dims, q_in, k_in, v_in, do_in, wide_in, lse_in, cos_ref, sin_ref, o_in, dx1b_in, h1_in, h2_ref, dy_ref, dy_full, y_ref,
                    wq_in, x_in, dx1t_in, sums_ref, vec_ref, wu_in, wd_in, h2_low, dy_cross,
                    y_out, gwo_ref, gx_ref, gwq_ref, gb_out, sums_out, gwu_ref, gbu_ref, gwd_ref, h2_high, dy_all,
                    dqkv_ref, gb_ref, h1_ref, near_buf, far_buf, near_gwq, far_gwq, near_last, gb_rows, gb_buf, sums_mine, sums_buf, gx_seq,
                    own_sem, load_sem, first_sem, tail_sem, red_send, red_recv, small_send, small_recv, h2_send, h2_recv, dy_send, dy_recv, y_send, y_recv, gx_send, gx_recv):
    local_heads, head_dim = dims
    me = lax.axis_index('tp')
    tp, chunk, width = dy_ref.shape
    half = head_dim // 2
    group = local_heads * head_dim
    rows = 3 * group
    seq_len = tp * chunk
    low_rows = h2_low.shape[1]
    mine, across, partner = rows_of(me, chunk), rows_of(me ^ 2, chunk), me ^ 1
    greet(me)
    h2_move = Gather(h2_ref.at[low_rows:], h2_high, 1, h2_send, h2_recv, me)
    y_move = from_sequence(y_ref, y_out, y_send, y_recv, me, chunk)
    dy_near = Copies([remote(source, dst, dy_send.at[i], dy_recv.at[i], partner) for i, (source, dst) in enumerate((
        (dy_full, dy_all.at[0]), (dy_ref.at[me ^ 2], dy_all.at[2, mine]), (dy_ref.at[me ^ 3], dy_all.at[1, mine])))])
    dy_relay = Copies([remote(dy_cross.at[i], dy_all.at[2 - i, across], dy_send.at[3 + i], dy_recv.at[3 + i], partner) for i in (0, 1)])
    own = Copies([pltpu.make_async_copy(dy_ref.at[me ^ 2], dy_all.at[1, mine], own_sem.at[0]), pltpu.make_async_copy(dy_ref.at[me ^ 3], dy_all.at[2, mine], own_sem.at[1]),
                  pltpu.make_async_copy(y_ref.at[mine], y_out.at[me], own_sem.at[2])]
                 + [pltpu.make_async_copy(dy_cross.at[i], dy_all.at[1 + i, across], own_sem.at[3 + i]) for i in (0, 1)])
    h2_move.start()
    y_move.start()
    dy_near.start()
    dy_relay.start()
    cos, sin = cos_ref[...], sin_ref[...]

    def store(m, j, which, low, high):
        grad = jnp.concatenate([low, high], axis=0)
        at = pl.ds(pl.multiple_of(which * group + j * head_dim, head_dim), head_dim)
        dqkv_ref[m, at] = grad.astype(BF16)
        gb_ref[m, at] = jnp.broadcast_to(lane_sum(grad), (head_dim, 128))

    def back(grad):
        low, high = grad[:half], grad[half:]
        return low * cos + high * sin, high * cos - low * sin

    def attention(q_all, k_all, v_all, do_ref, wide_ref, lse_ref, o_ref, dx1b_ref, part, part_gwq):
        def loads(m):
            heads = pl.ds(m * local_heads, local_heads)
            pairs = ((q_in, q_all), (k_in, k_all), (v_in, v_all), (do_in, do_ref), (wide_in, wide_ref), (lse_in, lse_ref))
            return Copies([pltpu.make_async_copy(source.at[heads], dst.at[heads], load_sem.at[i, m]) for i, (source, dst) in enumerate(pairs)])

        early = Copies([pltpu.make_async_copy(source, dst, first_sem.at[i]) for i, (source, dst) in enumerate(((o_in, o_ref), (dx1b_in, dx1b_ref), (h1_in, h1_ref)))])
        early.start()
        for m in range(tp - 1, -1, -1):
            loads(m).start()
        own.start()
        reduce_near = Copies([remote(part.at[source], near_buf.at[i], red_send.at[i], red_recv.at[i], partner) for i, source in enumerate((1, 3))])
        reduce_far = remote(part.at[2], far_buf, red_send.at[2], red_recv.at[2], me ^ 2)
        gwq_near = remote(part_gwq.at[1], near_gwq, red_send.at[3], red_recv.at[3], partner)
        gwq_far = remote(part_gwq.at[0], far_gwq, red_send.at[4], red_recv.at[4], me ^ 2)
        early.wait()
        part[...] = dot(o_ref[...].reshape(tp * group, seq_len), dx1b_ref[...]).reshape(part.shape)

        @pl.loop(0, tp * local_heads)
        def _(step):
            m = tp - 1 - lax.div(step, local_heads)
            j = lax.rem(step, local_heads)
            head = m * local_heads + j

            @pl.when(j == 0)
            def _():
                loads(m).wait()

            @pl.when(step == 1)
            def _():
                reduce_near.start()

            @pl.when(step == 3)
            def _():
                reduce_near.wait()
                part[0] += near_buf[0]
                part[2] += near_buf[1]

            @pl.when(step == 4)
            def _():
                reduce_far.start()

            @pl.when(step == 6)
            def _():
                h2_move.forward()

            @pl.when(step == 10)
            def _():
                for i in (0, 1):
                    part_gwq[i] = dot(dqkv_ref[2 + i], h1_ref[...])

            @pl.when(step == 11)
            def _():
                gwq_near.start()

            @pl.when(step == 12)
            def _():
                gwq_near.wait()
                part_gwq[0] += near_gwq[...]

            @pl.when(step == 13)
            def _():
                gwq_far.start()

            q, k, v, d_out = q_all[head], k_all[head], v_all[head], do_ref[head]
            delta = jnp.sum(d_out.astype(F32) * wide_ref[head], axis=0, keepdims=True)
            probs = jnp.exp(dot(k.T, q) - lse_ref[head])
            d_probs = dot(v.T, d_out)
            d_scores = (probs * (d_probs - delta)).astype(BF16)
            d_value = dot(probs.astype(BF16), d_out.T).T
            d_key = dot(d_scores, q[:head_dim].T).T
            d_query = dot(k[:head_dim], d_scores)
            low, high = back(d_query)
            scale = head_dim ** -0.5
            store(m, j, 0, low * scale, high * scale)
            low, high = back(d_key)
            store(m, j, 1, low, high)
            store(m, j, 2, d_value[:half], d_value[half:])

        own.wait()
        y_move.wait()
        h2_move.finish()
        dy_near.wait()
        dy_relay.wait()
        reduce_far.wait()
        gwo_ref[...] = part[0] + far_buf[...]
        gwq_far.wait_send()

    heads_all = tp * local_heads

    def vm(array):
        return pltpu.VMEM(array.shape, array.dtype)

    pl.run_scoped(attention, vm(q_in), vm(k_in), vm(v_in), vm(do_in), vm(wide_in), vm(lse_in), vm(o_in), vm(dx1b_in), pltpu.VMEM((tp, group, width), F32), pltpu.VMEM((2, rows, width), F32))

    def tail(wq_ref, x_ref, dx1t_ref, wu_ref, wd_ref, h2_all, dy_full_all, part, acc_up, acc_bias):
        first = [pltpu.make_async_copy(source, dst, tail_sem.at[i]) for i, (source, dst) in enumerate(((wq_in, wq_ref), (x_in, x_ref), (dx1t_in, dx1t_ref), (wu_in, wu_ref), (wd_in, wd_ref)))]
        for m in range(tp):
            if m == 0:
                first.append(pltpu.make_async_copy(h2_ref, h2_all.at[0], tail_sem.at[5]))
                first.append(pltpu.make_async_copy(dy_full, dy_full_all.at[0], tail_sem.at[6]))
            else:
                first.append(pltpu.make_async_copy(h2_low.at[m - 1], h2_all.at[m, :low_rows], tail_sem.at[4 + 3 * m]))
                first.append(pltpu.make_async_copy(h2_high.at[m - 1], h2_all.at[m, low_rows:], tail_sem.at[5 + 3 * m]))
                first.append(pltpu.make_async_copy(dy_all.at[m - 1], dy_full_all.at[m], tail_sem.at[6 + 3 * m]))
        for load in first:
            load.start()
        near = remote(part.at[1], near_last, red_send.at[5], red_recv.at[5], partner)
        part[...] = dot(dqkv_ref[:2].reshape(2 * rows, seq_len), h1_ref[...]).reshape(part.shape)
        cols = vec_ref[...].T
        gain, bias = cols[:, 4:5], cols[:, 5:6]
        first[0].wait()
        near.start()
        d_h1 = dot_tn(wq_ref[...].reshape(tp * rows, width), dqkv_ref[...].reshape(tp * rows, seq_len))
        for load in first[1:]:
            load.wait()
        _, x_hat, inv_std = layer_norm_rows(x_ref[...].T.astype(F32), gain, bias)
        grad_x = (dx1t_ref[...] + layer_norm_rows_grad(d_h1, x_hat, inv_std, gain)).astype(BF16)
        gx_seq[...] = grad_x.T
        sums = [lane_sum(d_h1 * x_hat), lane_sum(d_h1)]
        ln1 = jnp.concatenate(sums + [jnp.zeros((width, 126), F32)], axis=1).T
        sums_mine[...] = jnp.concatenate([sums_ref[:4], ln1[:4]], axis=0)
        gx_ref[me] = gx_seq[mine]
        for m in range(tp):
            gb_rows[m] = gb_ref[m].T[:8]
        small = [remote(gb_rows.at[m], gb_buf.at[m - 1], small_send.at[0, m], small_recv.at[0, m], me ^ m) for m in (1, 2, 3)]
        small += [remote(sums_mine, sums_buf.at[m - 1], small_send.at[1, m], small_recv.at[1, m], me ^ m) for m in (1, 2, 3)]
        for move in small:
            move.start()
        gx_move = from_sequence(gx_seq, gx_ref, gx_send, gx_recv, me, chunk)
        gx_move.start()
        acc_up[...] = jnp.zeros_like(acc_up)
        acc_bias[...] = jnp.zeros_like(acc_bias)
        gwd_ref[...] = jnp.zeros_like(gwd_ref)
        wu_t = wu_ref[...].T
        bu_col = cols[:, 6:7]

        @pl.loop(0, tp)
        def _(m):
            act, slope = gelu(dot_nt(wu_t, h2_all[m]) + bu_col)
            d_pre = dot_nt(wd_ref[...], dy_full_all[m]) * slope
            lanes = d_pre[:, :128]
            for i in range(1, seq_len // 128):
                lanes = lanes + d_pre[:, i * 128:(i + 1) * 128]
            acc_bias[...] += lanes
            gwd_ref[...] += dot(act, dy_full_all[m])
            acc_up[...] += dot(d_pre.astype(BF16), h2_all[m])

        gwu_ref[...] = acc_up[...].T
        gbu_ref[...] = jnp.broadcast_to(lane_sum(acc_bias[...]), acc_bias.shape).T[:8]
        near.wait()
        remote(part.at[0], far_gwq, red_send.at[4], red_recv.at[4], me ^ 2).wait_recv()
        gwq_ref[...] = part[0] + near_last[...] + far_gwq[...]
        for move in small:
            move.wait()
        gb_out[...] = gb_rows[0] + gb_buf[0] + (gb_buf[1] + gb_buf[2])
        sums_out[...] = sums_mine[...] + sums_buf[0] + (sums_buf[1] + sums_buf[2])
        gx_move.wait()

    pl.run_scoped(tail, vm(wq_in), vm(x_in), vm(dx1t_in), vm(wu_in), vm(wd_in), pltpu.VMEM((tp, seq_len, width), BF16), pltpu.VMEM((tp, seq_len, width), BF16),
                  pltpu.VMEM((2, rows, width), F32), pltpu.VMEM((wd_in.shape[0], width), F32), pltpu.VMEM((wd_in.shape[0], 128), F32))


VMEM_SPEC = pl.BlockSpec(memory_space=pltpu.VMEM)
ANY_SPEC = pl.BlockSpec(memory_space=pl.ANY)


def shape(dims, dtype=BF16):
    return jax.ShapeDtypeStruct(dims, dtype)


def single_call(kernel, name, collective_id, ins, in_any, outs, out_any, scratch):
    dma = pltpu.SemaphoreType.DMA
    return pl.pallas_call(
        kernel,
        out_shape=outs,
        in_specs=[ANY_SPEC if i in in_any else VMEM_SPEC for i in range(len(ins))],
        out_specs=[ANY_SPEC if i in out_any else VMEM_SPEC for i in range(len(outs))],
        scratch_shapes=[dma(s) if isinstance(s, tuple) else pltpu.VMEM(s.shape, s.dtype) for s in scratch],
        compiler_params=pltpu.CompilerParams(collective_id=collective_id, has_side_effects=True, vmem_limit_bytes=67043328),
        name=name,
    )(*ins)


def solution(mesh):
    tp = mesh.shape['tp']
    act_spec = P('dp', 'tp', None)
    rep_vec = P(None)
    part_vec = P('dp')
    in_specs = (act_spec, act_spec, P('dp', None), rep_vec, rep_vec, P(None, None, 'tp', None), P(None, 'tp', None),
                P('tp', None, None), rep_vec, rep_vec, rep_vec, P(None, 'tp'), P('tp'), P('tp', None), rep_vec)
    out_specs = (act_spec, act_spec, part_vec, part_vec, P('dp', None, 'tp', None), P('dp', 'tp', None),
                 P(('dp', 'tp'), None, None), part_vec, part_vec, part_vec, P('dp', 'tp'), P(('dp', 'tp')),
                 P(('dp', 'tp'), None), part_vec)

    def device_step(x_in, grad_y, pad_mask, ln1_gain, ln1_bias, w_qkv, b_qkv, w_out, b_out, ln2_gain, ln2_bias, w_up, b_up, w_down, b_down):
        seq_len = pad_mask.shape[1]
        local_heads, head_dim = w_qkv.shape[2:]
        chunk, width = x_in.shape[1:]
        ff = w_up.shape[1]
        heads = local_heads * tp
        group = local_heads * head_dim
        qkv_rows = 3 * group
        ext = head_dim + head_dim // 2
        low_rows = seq_len // 2
        dims = (local_heads, head_dim)
        cos_tab, sin_tab = (jnp.asarray(table) for table in rope_tables(seq_len, head_dim))
        wq_own = w_qkv.transpose(0, 2, 3, 1).reshape(2, qkv_rows // 2, width)
        bq_own = jnp.broadcast_to(b_qkv.reshape(1, qkv_rows), (8, qkv_rows))
        wo_own = w_out.reshape(2, group // 2, width)
        wu_own = w_up.reshape(2, width // 2, ff)
        wd_own = w_down.reshape(2, ff // 2, width)
        vec = jnp.stack([b_out, ln2_gain, ln2_bias, b_down, ln1_gain, ln1_bias, b_up, b_up])
        act = shape((seq_len, width))
        by_head = shape((heads, head_dim, seq_len))
        ext_head = shape((heads, ext, seq_len))
        held = [act, shape((tp,) + wq_own.shape), act, ext_head, ext_head, by_head, by_head, shape(by_head.shape, F32), shape((heads, 1, seq_len), F32)]
        d_x1_t = shape((width, seq_len), F32)
        rows8 = shape((8, width), F32)
        ins = (x_in, wq_own, bq_own, pad_mask, vec, cos_tab, sin_tab, wo_own, wu_own, wd_own, grad_y)
        outs = held + [act, act, d_x1_t, act, by_head, act, shape((tp - 1, low_rows, width)), shape((2, chunk, width)), rows8]
        scratch = held + [shape((width, seq_len)), shape((tp,) + bq_own.shape, F32), shape((tp,) + wo_own.shape), shape((tp,) + wu_own.shape), shape((tp,) + wd_own.shape), shape((tp,) + vec.shape, F32), act,
                          shape((tp, ff, seq_len)), shape((3, seq_len, width)), d_x1_t, (6,), (11,), (6, 4), (4,), (4,), (6,), (6,), (3, 3), (3, 3), (4, 5), (4, 5)]
        (x_full, wq_all, h1, q_ext, k_ext, v_heads, attn_o, attn_wide, lse, y_seq, h2, dx1_t, dx1_b, d_o, dy_full, h2_low, dy_cross, mid_sums) = single_call(
            functools.partial(forward_kernel, (chunk,) + dims), 'forward', 0, ins, (0, 1, 2, 4, 7, 8, 9, 10), outs, range(17), scratch)
        ins = (q_ext, k_ext, v_heads, d_o, attn_wide, lse, cos_tab, sin_tab, attn_o, dx1_b, h1, h2, grad_y, dy_full, y_seq, wq_all.reshape(tp, qkv_rows, width), x_full, dx1_t, mid_sums, vec, w_up, w_down, h2_low, dy_cross)
        gwq = shape((qkv_rows, width), F32)
        gwo = shape((group, width), F32)
        outs = [shape((tp, chunk, width)), gwo, shape((tp, chunk, width)), gwq, shape((8, qkv_rows), F32), rows8, shape(w_up.shape, F32), shape((8, ff), F32), shape(w_down.shape, F32),
                shape((tp - 1, seq_len - low_rows, width)), shape((tp - 1, seq_len, width))]
        scratch = [shape((tp, qkv_rows, seq_len)), shape((tp, qkv_rows, 128), F32), act, shape((2, group, width), F32), gwo, gwq, gwq, gwq, shape((tp, 8, qkv_rows), F32), shape((3, 8, qkv_rows), F32), rows8, shape((3, 8, width), F32), act,
                   (5,), (6, 4), (3,), (16,), (6,), (6,), (2, 4), (2, 4), (3,), (3,), (5,), (5,), (4,), (4,), (4,), (4,)]
        y_out, grad_w_out, grad_x, grad_w_qkv, grad_b_qkv, sums, grad_w_up, grad_b_up, grad_w_down, _, _ = single_call(
            functools.partial(backward_kernel, dims), 'backward', 1, ins, (0, 1, 2, 3, 4, 5, 8, 9, 10, 11, 12, 13, 14, 15, 16, 17, 20, 21, 22, 23), outs, (0, 9, 10), scratch)
        grad_w_qkv = grad_w_qkv.reshape(3, local_heads, head_dim, width).transpose(0, 3, 1, 2)
        grad_b_qkv = grad_b_qkv[0].reshape(3, local_heads, head_dim)
        grad_w_out = grad_w_out.reshape(local_heads, head_dim, width)
        return (y_out, grad_x, sums[4], sums[5], grad_w_qkv, grad_b_qkv, grad_w_out, sums[3],
                sums[1], sums[2], grad_w_up, grad_b_up[0], grad_w_down, sums[0])

    return jax.shard_map(device_step, mesh=mesh, in_specs=in_specs, out_specs=out_specs, check_vma=False)
```

time: 837 us -> 223 us (0.27)
  waiting for transfers between devices: 419 us -> 0 us
  matrix products: 270 us -> 0 us
  Pallas kernels: 0 us -> 202 us
  other arithmetic: 100 us -> 0 us
  between operations: 15.2 us -> 0.68 us
  blocking collectives: 10.1 us -> 0 us
    reduce_scatter x4 -> x0, waiting for transfers between devices: 275 us -> none  [the longest x1 77.6 us: device_step(): lax.psum_scatter(attn_part, 'tp', scatter_dimension=1, tiled=True)]
    dot_general x17 -> x0, matrix products: 235 us -> none  [the longest x1 54.2 us: device_step(): jnp.einsum('bqhk,bshk->bhqs', d_attn_o, v_heads, preferred_element_type=j...]
    pallas_call x0 -> x2, Pallas kernels: none -> 202 us  [single_call(): pl.pallas_call(kernel, out_shape=outs, in_specs=[ANY_SPEC if i in in_any...]
    all_gather x4 -> x0, waiting for transfers between devices: 143 us -> none  [the longest x1 39.4 us: device_step(): lax.all_gather(h1_f.astype(jnp.bfloat16), 'tp', axis=1, tiled=True)]
    convert_element_type x6 -> x0, other arithmetic: 75.9 us -> none  [the longest x1 65.3 us: device_step(): (attn_probs * (d_probs - jnp.sum(d_probs * attn_probs, axis=-1, keepdims=...]
    sub x1 -> x0, matrix products: 35.2 us -> none  [device_step(): attn_probs = jax.nn.softmax(jnp.where(key_ok, scores, NEG_LARGE), axis=-1)]
    reduce_sum x8 -> x0, other arithmetic: 17.7 us -> none  [the longest x1 4.7 us: device_step(): jnp.sum(d_x1, axis=(0, 1))]
    psum x1 -> x0, blocking collectives: 10.1 us -> none  [device_step(): lax.psum(jnp.stack([jnp.sum(d_h1 * x_hat1, axis=(0, 1)), jnp.sum(d_h1, ax...]
  transfers between devices with their start and end apart: 8 -> 0, of which waited for: 8 -> 0; matrix products, arithmetic and copies ran while one was open for 6% -> 0% of each run, Pallas kernels for 0% -> 0%
where the time goes in v2:
time: 223 us; the launch traced here: 222 us
  Pallas kernels  202 us (91%)
  local copies, waits for them, and re-layouts  19.5 us (9%)
    pallas_call x2, Pallas kernels, single_call(): pl.pallas_call(kernel, out_shape=outs, in_specs=[ANY_SPEC if i in in_any...  202 us
    unnamed x18, local copies, waits for them, and re-layouts  10.9 us
    another operation x8, local copies, waits for them, and re-layouts, device_step(): jnp.stack([b_out, ln2_gain, ln2_bias, b_down, ln1_gain, ln1_bias, b_up, b...  5.46 us

profile of v2, /device:TPU:0, one launch (start us, length us, event | category | flops | bytes accessed | tf_op | source)
XLA Modules:
  0.0 222.3 jit_solution(10377036452751842466)
XLA Ops:
  0.6 0.7 stack.29
  1.3 0.7 stack.30
  2.0 0.7 stack.25
  2.7 0.7 stack.26
  3.4 0.7 stack.27
  4.1 0.7 stack.31
  4.8 0.7 stack.28
  5.5 0.6 stack.32.vec_ref
  6.1 0.7 copy.32
  6.8 0.1 broadcast_in_dim.7
  6.9 0.6 broadcast_in_dim.8.bq_ref
  7.5 99.3 %forward.1 = (bf16[1024,640]{1,0:T(8,128)(2,1)}, bf16[4,2,240,640]{3,2,1,0:T(8,128)(2,1)}, bf16[1024,640]{1,0:T(8,128)(2,1)}, bf16[20,48,1024]{2,1,0:T(8,128)(2,...) custom-call(bf16[4,256,640]{2,1,0:T(8,128)(2,1)} %x_ref.1, ...), custom_call_target="tpu_custom_call" | custom-call | tf_op jit(solution)/shard_map/forward/pallas_call | solution.py:563
  106.8 102.8 %backward.1 = (bf16[4,256,640]{2,1,0:T(8,128)(2,1)}, f32[160,640]{1,0:T(8,128)}, bf16[4,256,640]{2,1,0:T(8,128)(2,1)}, f32[480,640]{1,0:T(8,128)}, f32[8,480]{1,...) custom-call(bf16[20,48,1024]{2,1,0:T(8,128)(2,1)} %get-tuple-element, ...), custom_call_target="tpu_custom_call" | custom-call | tf_op jit(solution)/shard_map/backward/pallas_call | solution.py:563
  209.6 0.7 slice_reduce_fusion.7
  210.3 0.1 reshape_squeeze.3
  210.4 0.6 copy.33
  211.0 1.7 slice_reduce_fusion
  212.7 0.0 copy-start.2
  212.7 2.6 %copy.40 = bf16[4,256,640]{2,1,0:T(8,128)(2,1)} copy(bf16[4,256,640]{2,1,0:T(8,128)(2,1)} %get-tuple-element.117) | data formatting | bytes 2621440
  215.3 0.0 copy-done.2
  215.3 0.0 copy-start.3
  215.3 1.1 copy.41
  216.4 0.7 copy-done.3
  217.1 0.0 copy-start.4
  217.1 0.0 copy-start.1
  217.1 1.0 copy.42
  218.1 0.2 copy-done.4
  218.3 0.8 copy.43
  219.1 0.0 copy-done.1
  219.1 0.0 copy-start
  219.1 1.2 copy.44
  220.2 0.9 copy-done
  221.1 1.2 copy.45
Async XLA Ops:
  212.7 2.6 %copy-start.2 = (bf16[4,256,640]{2,1,0:T(8,128)(2,1)S(1)}, bf16[4,256,640]{2,1,0:T(8,128)(2,1)}, u32[]{:S(2)}) copy-start(bf16[4,256,640]{2,1,0:T(8,128)(2,1)} %get-tuple-element.118) | copy-start | bytes 3932164
  215.3 1.8 copy-start.3
  217.1 1.3 copy-start.4
  217.1 2.0 copy-start.1
  219.1 2.0 copy-start

commit v3 on v2

--- a/solution.py
+++ b/solution.py
@@ -159,8 +159,8 @@
     return jnp.sum(value, axis=1, keepdims=True)
 
 
-def forward_kernel(dims, x_ref, wq_ref, bq_ref, mask_ref, vec_ref, cos_ref, sin_ref, wo_ref, wu_ref, wd_ref, dy_ref,
-                   x_out, wq_out, h1_out, q_out, k_out, v_out, o_out, wide_out, lse_out, y_out, h2_out, dx1t_out, dx1b_out, do_out, dy_out, h2_all, dy_cross, sums_ref,
+def forward_kernel(dims, x_ref, wq_ref, bq_ref, mask_ref, b_out_ref, gain2_ref, bias2_ref, b_down_ref, gain1_ref, bias1_ref, b_up_ref, cos_ref, sin_ref, wo_ref, wu_ref, wd_ref, dy_ref,
+                   x_out, wq_out, h1_out, q_out, k_out, v_out, o_out, wide_out, lse_out, y_out, h2_out, dx1t_out, dx1b_out, do_out, dy_out, h2_all, dy_cross, sums_ref, vec_ref,
                    x_full, wq_all, h1_ref, q_all, k_all, v_all, o_ref, wide_ref, lse_ref, h1t_ref, bq_all, wo_all, wu_all, wd_all, vec_all, dy_full,
                    act_ref, stage_ref, wide_stage, own_sem, once_sem, store_sem, x_send, x_recv, dy_send, dy_recv, send_sem, recv_sem, wide_send, wide_recv):
     chunk, local_heads, head_dim = dims
@@ -168,17 +168,20 @@
     half = head_dim // 2
     seq_len, width = x_full.shape
     tp, ff = wu_all.shape[0], wu_ref.shape[2]
+    for i, row in enumerate((b_out_ref, gain2_ref, bias2_ref, b_down_ref, gain1_ref, bias1_ref, b_up_ref, b_up_ref)):
+        vec_ref[i:i + 1] = row[...].reshape(1, width)
     greet(me, True)
     x_move = to_sequence(x_ref, x_full, x_send, x_recv, me, chunk)
     dy_move = to_sequence(dy_ref, dy_full, dy_send, dy_recv, me, chunk)
     dy_far = Copies([remote(dy_ref.at[me ^ i], dy_cross.at[i], dy_send.at[4 + i], dy_recv.at[4 + i], me ^ 2) for i in (0, 1)])
+    vec_all[0] = vec_ref[...]
     gathered = ((bq_ref, bq_all), (vec_ref, vec_all))
     moves = [Gather(source, dst, 0, send_sem.at[i], recv_sem.at[i], me) for i, (source, dst) in enumerate(gathered)]
     bq, vec = moves
     weights = ((wq_ref, wq_all), (wo_ref, wo_all), (wu_ref, wu_all), (wd_ref, wd_all))
     shared = [SharedGather(source, dst, wide_send.at[i], wide_recv.at[i], me) for i, (source, dst) in enumerate(weights)]
     wq, wo, wu, wd = shared
-    own = [pltpu.make_async_copy(source, dst.at[0], own_sem.at[i]) for i, (source, dst) in enumerate(gathered + weights)]
+    own = [pltpu.make_async_copy(source, dst.at[0], own_sem.at[i]) for i, (source, dst) in enumerate(gathered[:1] + weights)]
     x_move.start()
     bq.start()
     wq.start()
@@ -237,26 +240,27 @@
             wu.forward()
             wd.forward()
 
-        bias = bq_all[m].T[:, :1]
-        qkv = dot(wq_all[m].reshape(bias.shape[0], width), h1t_ref[...]) + bias
+        biases = [bq_all[m, j].T for j in range(local_heads)]
+        qkv = dot(wq_all[m].reshape(3 * local_heads * head_dim, width), h1t_ref[...])
         cos, sin = cos_ref[...], sin_ref[...]
         group = local_heads * head_dim
         for j in range(local_heads):
             head = m * local_heads + j
             for which, (dst, scale, extra) in enumerate(((q_all, head_dim ** -0.5, ones), (k_all, None, key_bias))):
-                rows = qkv[which * group + j * head_dim:which * group + (j + 1) * head_dim]
+                rows = qkv[which * group + j * head_dim:which * group + (j + 1) * head_dim] + biases[j][:, which:which + 1]
                 rows = rows * scale if scale is not None else rows
                 low, high = rows[:half], rows[half:]
                 dst[head, :half] = (low * cos - high * sin).astype(BF16)
                 dst[head, half:head_dim] = (high * cos + low * sin).astype(BF16)
                 dst[head, head_dim:] = extra
-            v_all[head] = qkv[2 * group + j * head_dim:2 * group + (j + 1) * head_dim].astype(BF16)
-
-        @pl.loop(0, local_heads)
-        def _(j):
-            head = m * local_heads + j
-            scores = dot(k_all[head].T, q_all[head])
+            v_all[head] = (qkv[2 * group + j * head_dim:2 * group + (j + 1) * head_dim] + biases[j][:, 2:3]).astype(BF16)
+
+        coming = dot(k_all[m * local_heads].T, q_all[m * local_heads])
+        for j in range(local_heads):
+            head, scores = m * local_heads + j, coming
             top = jnp.max(scores, axis=0, keepdims=True)
+            if j + 1 < local_heads:
+                coming = dot(k_all[head + 1].T, q_all[head + 1])
             weights = jnp.exp(scores - top)
             total = jnp.sum(weights, axis=0, keepdims=True)
             out = dot(v_all[head], weights.astype(BF16)) / total
@@ -305,6 +309,7 @@
         dy_move.wait_recv()
         once[7].start()
         dy_t = dy_full[...].T
+        wide_stage[...] = jnp.zeros_like(wide_stage)
 
         @pl.loop(0, tp)
         def _(m):
@@ -312,12 +317,11 @@
             def _():
                 once[4].start()
 
-            act_ref[m] = (dot(wd_all[m].reshape(ff, width), dy_t) * slope_ref[m]).astype(BF16)
+            d_pre = (dot(wd_all[m].reshape(ff, width), dy_t) * slope_ref[m]).astype(BF16)
+            wide_stage[...] += dot(wu_all[m].reshape(width, ff), d_pre)
 
     pl.run_scoped(mlp, pltpu.VMEM((tp, ff, seq_len), F32))
-    d_h2 = dot(wu_all[0].reshape(width, ff), act_ref[0])
-    for m in range(1, tp):
-        d_h2 = d_h2 + dot(wu_all[m].reshape(width, ff), act_ref[m])
+    d_h2 = wide_stage[...]
     dy_f = dy_full[...].T.astype(F32)
     d_x1 = dy_f + layer_norm_rows_grad(d_h2, x_hat, inv_std, gain)
     d_x1_b = d_x1.astype(BF16)
@@ -403,7 +407,11 @@
         gwq_near = remote(part_gwq.at[1], near_gwq, red_send.at[3], red_recv.at[3], partner)
         gwq_far = remote(part_gwq.at[0], far_gwq, red_send.at[4], red_recv.at[4], me ^ 2)
         early.wait()
-        part[...] = dot(o_ref[...].reshape(tp * group, seq_len), dx1b_ref[...]).reshape(part.shape)
+
+        @pl.loop(0, tp)
+        def _(m):
+            heads = pl.ds(m * local_heads, local_heads)
+            part[m] = dot(o_ref[heads].reshape(group, seq_len), dx1b_ref[...])
 
         @pl.loop(0, tp * local_heads)
         def _(step):
@@ -435,7 +443,8 @@
 
             @pl.when(step == 10)
             def _():
-                for i in (0, 1):
+                @pl.loop(0, 2)
+                def _(i):
                     part_gwq[i] = dot(dqkv_ref[2 + i], h1_ref[...])
 
             @pl.when(step == 11)
@@ -495,7 +504,11 @@
         for load in first:
             load.start()
         near = remote(part.at[1], near_last, red_send.at[5], red_recv.at[5], partner)
-        part[...] = dot(dqkv_ref[:2].reshape(2 * rows, seq_len), h1_ref[...]).reshape(part.shape)
+
+        @pl.loop(0, 2)
+        def _(i):
+            part[i] = dot(dqkv_ref[i], h1_ref[...])
+
         cols = vec_ref[...].T
         gain, bias = cols[:, 4:5], cols[:, 5:6]
         first[0].wait()
@@ -550,6 +563,31 @@
                   pltpu.VMEM((2, rows, width), F32), pltpu.VMEM((wd_in.shape[0], width), F32), pltpu.VMEM((wd_in.shape[0], 128), F32))
 
 
+def finish_kernel(*refs):
+    moved, small = refs[:6], refs[6:9]
+    outs, vectors, bias_up, bias_qkv = refs[9:15], refs[15:21], refs[21], refs[22]
+    bufs, load_sem, store_sem = refs[23:29], refs[29], refs[30]
+    loads = [pltpu.make_async_copy(source, buf, load_sem.at[i]) for i, (source, buf) in enumerate(zip(moved, bufs))]
+    stores = [pltpu.make_async_copy(buf, dst, store_sem.at[i]) for i, (buf, dst) in enumerate(zip(bufs, outs))]
+    for load in loads:
+        load.start()
+    for load, store in zip(loads, stores):
+        load.wait()
+        store.start()
+    sums, grad_up, grad_qkv = small
+    for i, vector in enumerate(vectors):
+        vector[...] = sums[i]
+    bias_up[...] = grad_up[0]
+    heads, kinds, head_dim = bias_qkv.shape
+    row = grad_qkv[:1]
+    for j in range(heads):
+        for which in range(kinds):
+            at = (which * heads + j) * head_dim
+            bias_qkv[j, which:which + 1] = row[:, at:at + head_dim]
+    for store in stores:
+        store.wait()
+
+
 VMEM_SPEC = pl.BlockSpec(memory_space=pltpu.VMEM)
 ANY_SPEC = pl.BlockSpec(memory_space=pl.ANY)
 
@@ -558,7 +596,7 @@
     return jax.ShapeDtypeStruct(dims, dtype)
 
 
-def single_call(kernel, name, collective_id, ins, in_any, outs, out_any, scratch):
+def single_call(kernel, name, collective_id, ins, in_any, outs, out_any, scratch, limit=67043328):
     dma = pltpu.SemaphoreType.DMA
     return pl.pallas_call(
         kernel,
@@ -566,7 +604,7 @@
         in_specs=[ANY_SPEC if i in in_any else VMEM_SPEC for i in range(len(ins))],
         out_specs=[ANY_SPEC if i in out_any else VMEM_SPEC for i in range(len(outs))],
         scratch_shapes=[dma(s) if isinstance(s, tuple) else pltpu.VMEM(s.shape, s.dtype) for s in scratch],
-        compiler_params=pltpu.CompilerParams(collective_id=collective_id, has_side_effects=True, vmem_limit_bytes=67043328),
+        compiler_params=pltpu.CompilerParams(collective_id=collective_id, has_side_effects=collective_id is not None, vmem_limit_bytes=limit),
         name=name,
     )(*ins)
 
@@ -591,27 +629,26 @@
         group = local_heads * head_dim
         qkv_rows = 3 * group
         ext = head_dim + head_dim // 2
-        low_rows = seq_len // 2
+        low_rows = seq_len // 4
         dims = (local_heads, head_dim)
         cos_tab, sin_tab = (jnp.asarray(table) for table in rope_tables(seq_len, head_dim))
         wq_own = w_qkv.transpose(0, 2, 3, 1).reshape(2, qkv_rows // 2, width)
-        bq_own = jnp.broadcast_to(b_qkv.reshape(1, qkv_rows), (8, qkv_rows))
+        bq_own = b_qkv.transpose(1, 0, 2)
         wo_own = w_out.reshape(2, group // 2, width)
         wu_own = w_up.reshape(2, width // 2, ff)
         wd_own = w_down.reshape(2, ff // 2, width)
-        vec = jnp.stack([b_out, ln2_gain, ln2_bias, b_down, ln1_gain, ln1_bias, b_up, b_up])
         act = shape((seq_len, width))
         by_head = shape((heads, head_dim, seq_len))
         ext_head = shape((heads, ext, seq_len))
         held = [act, shape((tp,) + wq_own.shape), act, ext_head, ext_head, by_head, by_head, shape(by_head.shape, F32), shape((heads, 1, seq_len), F32)]
         d_x1_t = shape((width, seq_len), F32)
         rows8 = shape((8, width), F32)
-        ins = (x_in, wq_own, bq_own, pad_mask, vec, cos_tab, sin_tab, wo_own, wu_own, wd_own, grad_y)
-        outs = held + [act, act, d_x1_t, act, by_head, act, shape((tp - 1, low_rows, width)), shape((2, chunk, width)), rows8]
-        scratch = held + [shape((width, seq_len)), shape((tp,) + bq_own.shape, F32), shape((tp,) + wo_own.shape), shape((tp,) + wu_own.shape), shape((tp,) + wd_own.shape), shape((tp,) + vec.shape, F32), act,
-                          shape((tp, ff, seq_len)), shape((3, seq_len, width)), d_x1_t, (6,), (11,), (6, 4), (4,), (4,), (6,), (6,), (3, 3), (3, 3), (4, 5), (4, 5)]
-        (x_full, wq_all, h1, q_ext, k_ext, v_heads, attn_o, attn_wide, lse, y_seq, h2, dx1_t, dx1_b, d_o, dy_full, h2_low, dy_cross, mid_sums) = single_call(
-            functools.partial(forward_kernel, (chunk,) + dims), 'forward', 0, ins, (0, 1, 2, 4, 7, 8, 9, 10), outs, range(17), scratch)
+        ins = (x_in, wq_own, bq_own, pad_mask, b_out, ln2_gain, ln2_bias, b_down, ln1_gain, ln1_bias, b_up, cos_tab, sin_tab, wo_own, wu_own, wd_own, grad_y)
+        outs = held + [act, act, d_x1_t, act, by_head, act, shape((tp - 1, low_rows, width)), shape((2, chunk, width)), rows8, rows8]
+        scratch = held + [shape((width, seq_len)), shape((tp,) + bq_own.shape, F32), shape((tp,) + wo_own.shape), shape((tp,) + wu_own.shape), shape((tp,) + wd_own.shape), shape((tp,) + rows8.shape, F32), act,
+                          shape((tp, ff, seq_len)), shape((3, seq_len, width)), d_x1_t, (5,), (11,), (6, 4), (4,), (4,), (6,), (6,), (3, 3), (3, 3), (4, 5), (4, 5)]
+        (x_full, wq_all, h1, q_ext, k_ext, v_heads, attn_o, attn_wide, lse, y_seq, h2, dx1_t, dx1_b, d_o, dy_full, h2_low, dy_cross, mid_sums, vec) = single_call(
+            functools.partial(forward_kernel, (chunk,) + dims), 'forward', 0, ins, (0, 1, 2, 13, 14, 15, 16), outs, range(17), scratch)
         ins = (q_ext, k_ext, v_heads, d_o, attn_wide, lse, cos_tab, sin_tab, attn_o, dx1_b, h1, h2, grad_y, dy_full, y_seq, wq_all.reshape(tp, qkv_rows, width), x_full, dx1_t, mid_sums, vec, w_up, w_down, h2_low, dy_cross)
         gwq = shape((qkv_rows, width), F32)
         gwo = shape((group, width), F32)
@@ -621,10 +658,17 @@
                    (5,), (6, 4), (3,), (16,), (6,), (6,), (2, 4), (2, 4), (3,), (3,), (5,), (5,), (4,), (4,), (4,), (4,)]
         y_out, grad_w_out, grad_x, grad_w_qkv, grad_b_qkv, sums, grad_w_up, grad_b_up, grad_w_down, _, _ = single_call(
             functools.partial(backward_kernel, dims), 'backward', 1, ins, (0, 1, 2, 3, 4, 5, 8, 9, 10, 11, 12, 13, 14, 15, 16, 17, 20, 21, 22, 23), outs, (0, 9, 10), scratch)
+        moved = (y_out, grad_x, grad_w_qkv, grad_w_out, grad_w_up, grad_w_down)
+        ins = moved + (sums, grad_b_up, grad_b_qkv)
+        vector = shape((width,), F32)
+        moved_shapes = [shape(a.shape, a.dtype) for a in moved]
+        outs = moved_shapes + [vector] * 6 + [shape((ff,), F32), shape((local_heads, 3, head_dim), F32)]
+        y_out, grad_x, grad_w_qkv, grad_w_out, grad_w_up, grad_w_down, *vectors, grad_b_up, grad_b_qkv = single_call(
+            finish_kernel, 'finish', None, ins, range(6), outs, range(6), moved_shapes + [(6,), (6,)])
         grad_w_qkv = grad_w_qkv.reshape(3, local_heads, head_dim, width).transpose(0, 3, 1, 2)
-        grad_b_qkv = grad_b_qkv[0].reshape(3, local_heads, head_dim)
+        grad_b_qkv = grad_b_qkv.transpose(1, 0, 2)
         grad_w_out = grad_w_out.reshape(local_heads, head_dim, width)
-        return (y_out, grad_x, sums[4], sums[5], grad_w_qkv, grad_b_qkv, grad_w_out, sums[3],
-                sums[1], sums[2], grad_w_up, grad_b_up[0], grad_w_down, sums[0])
+        return (y_out, grad_x, vectors[4], vectors[5], grad_w_qkv, grad_b_qkv, grad_w_out, vectors[3],
+                vectors[1], vectors[2], grad_w_up, grad_b_up, grad_w_down, vectors[0])
 
     return jax.shard_map(device_step, mesh=mesh, in_specs=in_specs, out_specs=out_specs, check_vma=False)

time: 223 us -> 209 us (0.937)
  local copies, waits for them, and re-layouts: 19.5 us -> 0 us
  Pallas kernels: 202 us -> 208 us
    unnamed x18 -> x0, local copies, waits for them, and re-layouts: 10.9 us -> none
    pallas_call x2 -> x3, Pallas kernels: 202 us -> 208 us  [single_call(): pl.pallas_call(kernel, out_shape=outs, in_specs=[ANY_SPEC if i in in_any...]
    another operation x9 -> x0, local copies, waits for them, and re-layouts: 5.54 us -> none  [the longest x8 5.46 us: device_step(): jnp.stack([b_out, ln2_gain, ln2_bias, b_down, ln1_gain, ln1_bias, b_up, b...]
    slice x2 -> x0, local copies, waits for them, and re-layouts: 2.42 us -> none  [the longest x1 1.68 us: device_step(): sums[0]]
where the time goes in v3:
time: 209 us
  Pallas kernels  208 us (100%)
    pallas_call x3, Pallas kernels, single_call(): pl.pallas_call(kernel, out_shape=outs, in_specs=[ANY_SPEC if i in in_any...  208 us

profile of v3, /device:TPU:0, one launch (start us, length us, event | category | flops | bytes accessed | tf_op | source)
XLA Modules:
  0.0 209.1 jit_solution(4396717492470074689)
XLA Ops:
  0.6 94.8 %forward.1 = (bf16[1024,640]{1,0:T(8,128)(2,1)}, bf16[4,2,240,640]{3,2,1,0:T(8,128)(2,1)}, bf16[1024,640]{1,0:T(8,128)(2,1)}, bf16[20,48,1024]{2,1,0:T(8,128)(2,...) custom-call(bf16[4,256,640]{2,1,0:T(8,128)(2,1)} %x_ref.1, ...), custom_call_target="tpu_custom_call" | custom-call | tf_op jit(solution)/shard_map/forward/pallas_call | solution.py:601
  95.5 106.0 %backward.1 = (bf16[4,256,640]{2,1,0:T(8,128)(2,1)}, f32[160,640]{1,0:T(8,128)}, bf16[4,256,640]{2,1,0:T(8,128)(2,1)}, f32[480,640]{1,0:T(8,128)}, f32[8,480]{1,...) custom-call(bf16[20,48,1024]{2,1,0:T(8,128)(2,1)} %get-tuple-element, ...), custom_call_target="tpu_custom_call" | custom-call | tf_op jit(solution)/shard_map/backward/pallas_call | solution.py:601
  201.5 7.4 %finish.1 = (bf16[4,256,640]{2,1,0:T(8,128)(2,1)}, bf16[4,256,640]{2,1,0:T(8,128)(2,1)}, f32[480,640]{1,0:T(8,128)}, f32[160,640]{1,0:T(8,128)}, f32[640,640]{1,...) custom-call(bf16[4,256,640]{2,1,0:T(8,128)(2,1)} %get-tuple-element., ...), custom_call_target="tpu_custom_call" | custom-call | tf_op jit(solution)/shard_map/finish/pallas_call | solution.py:601

commit v4 on v3

--- a/solution.py
+++ b/solution.py
@@ -187,8 +187,8 @@
     wq.start()
     for copy in own:
         copy.start()
-    for move in (vec, wo, wu, wd, dy_move, dy_far):
-        move.start()
+    vec.start()
+    wo.start()
     own_rows = rows_of(me, chunk)
     own_x = pltpu.make_async_copy(x_ref.at[me], x_full.at[own_rows], once_sem.at[0])
     own_dy = pltpu.make_async_copy(dy_ref.at[me], dy_full.at[own_rows], once_sem.at[1])
@@ -202,6 +202,8 @@
         copy.wait()
     own_x.wait()
     x_move.wait_recv()
+    for move in (wu, wd, dy_move, dy_far):
+        move.start()
     h1, _, _ = layer_norm(x_full[...].astype(F32), vec_all[0, 4:5], vec_all[0, 5:6])
     h1 = h1.astype(BF16)
     h1_ref[...] = h1
@@ -230,6 +232,7 @@
             wq.forward_rest()
             vec.forward()
             wo.forward()
+            wu.forward()
 
         @pl.when(m == 3)
         def _():
@@ -237,7 +240,6 @@
             wq.relay.wait_recv()
             once[2].start()
             wo.forward_rest()
-            wu.forward()
             wd.forward()
 
         biases = [bq_all[m, j].T for j in range(local_heads)]
@@ -271,7 +273,6 @@
         stores(m).start()
 
     wu.forward_rest()
-    wd.forward_rest()
     for move in (vec, wo):
         move.near.wait_recv()
         move.relay.wait_recv()
@@ -293,6 +294,7 @@
         def _(m):
             @pl.when(m == 1)
             def _():
+                wd.forward_rest()
                 h2_move.start()
                 once[3].start()
 
@@ -355,7 +357,7 @@
 def backward_kernel(dims, q_in, k_in, v_in, do_in, wide_in, lse_in, cos_ref, sin_ref, o_in, dx1b_in, h1_in, h2_ref, dy_ref, dy_full, y_ref,
                     wq_in, x_in, dx1t_in, sums_ref, vec_ref, wu_in, wd_in, h2_low, dy_cross,
                     y_out, gwo_ref, gx_ref, gwq_ref, gb_out, sums_out, gwu_ref, gbu_ref, gwd_ref, h2_high, dy_all,
-                    dqkv_ref, gb_ref, h1_ref, near_buf, far_buf, near_gwq, far_gwq, near_last, gb_rows, gb_buf, sums_mine, sums_buf, gx_seq,
+                    dqkv_ref, gb_ref, h1_ref, near_buf, far_buf, near_gwq, far_gwq, near_last, part_gwq, gb_rows, gb_buf, sums_mine, sums_buf, gx_seq,
                     own_sem, load_sem, first_sem, tail_sem, red_send, red_recv, small_send, small_recv, h2_send, h2_recv, dy_send, dy_recv, y_send, y_recv, gx_send, gx_recv):
     local_heads, head_dim = dims
     me = lax.axis_index('tp')
@@ -391,7 +393,7 @@
         low, high = grad[:half], grad[half:]
         return low * cos + high * sin, high * cos - low * sin
 
-    def attention(q_all, k_all, v_all, do_ref, wide_ref, lse_ref, o_ref, dx1b_ref, part, part_gwq):
+    def attention(q_all, k_all, v_all, do_ref, wide_ref, lse_ref, o_ref, dx1b_ref, part):
         def loads(m):
             heads = pl.ds(m * local_heads, local_heads)
             pairs = ((q_in, q_all), (k_in, k_all), (v_in, v_all), (do_in, do_ref), (wide_in, wide_ref), (lse_in, lse_ref))
@@ -437,7 +439,7 @@
             def _():
                 reduce_far.start()
 
-            @pl.when(step == 6)
+            @pl.when(step == 9)
             def _():
                 h2_move.forward()
 
@@ -482,14 +484,13 @@
         dy_relay.wait()
         reduce_far.wait()
         gwo_ref[...] = part[0] + far_buf[...]
-        gwq_far.wait_send()
 
     heads_all = tp * local_heads
 
     def vm(array):
         return pltpu.VMEM(array.shape, array.dtype)
 
-    pl.run_scoped(attention, vm(q_in), vm(k_in), vm(v_in), vm(do_in), vm(wide_in), vm(lse_in), vm(o_in), vm(dx1b_in), pltpu.VMEM((tp, group, width), F32), pltpu.VMEM((2, rows, width), F32))
+    pl.run_scoped(attention, vm(q_in), vm(k_in), vm(v_in), vm(do_in), vm(wide_in), vm(lse_in), vm(o_in), vm(dx1b_in), pltpu.VMEM((tp, group, width), F32))
 
     def tail(wq_ref, x_ref, dx1t_ref, wu_ref, wd_ref, h2_all, dy_full_all, part, acc_up, acc_bias):
         first = [pltpu.make_async_copy(source, dst, tail_sem.at[i]) for i, (source, dst) in enumerate(((wq_in, wq_ref), (x_in, x_ref), (dx1t_in, dx1t_ref), (wu_in, wu_ref), (wd_in, wd_ref)))]
@@ -551,7 +552,7 @@
         gwu_ref[...] = acc_up[...].T
         gbu_ref[...] = jnp.broadcast_to(lane_sum(acc_bias[...]), acc_bias.shape).T[:8]
         near.wait()
-        remote(part.at[0], far_gwq, red_send.at[4], red_recv.at[4], me ^ 2).wait_recv()
+        remote(part_gwq.at[0], far_gwq, red_send.at[4], red_recv.at[4], me ^ 2).wait()
         gwq_ref[...] = part[0] + near_last[...] + far_gwq[...]
         for move in small:
             move.wait()
@@ -654,10 +655,10 @@
         gwo = shape((group, width), F32)
         outs = [shape((tp, chunk, width)), gwo, shape((tp, chunk, width)), gwq, shape((8, qkv_rows), F32), rows8, shape(w_up.shape, F32), shape((8, ff), F32), shape(w_down.shape, F32),
                 shape((tp - 1, seq_len - low_rows, width)), shape((tp - 1, seq_len, width))]
-        scratch = [shape((tp, qkv_rows, seq_len)), shape((tp, qkv_rows, 128), F32), act, shape((2, group, width), F32), gwo, gwq, gwq, gwq, shape((tp, 8, qkv_rows), F32), shape((3, 8, qkv_rows), F32), rows8, shape((3, 8, width), F32), act,
+        scratch = [shape((tp, qkv_rows, seq_len)), shape((tp, qkv_rows, 128), F32), act, shape((2, group, width), F32), gwo, gwq, gwq, gwq, shape((2, qkv_rows, width), F32), shape((tp, 8, qkv_rows), F32), shape((3, 8, qkv_rows), F32), rows8, shape((3, 8, width), F32), act,
                    (5,), (6, 4), (3,), (16,), (6,), (6,), (2, 4), (2, 4), (3,), (3,), (5,), (5,), (4,), (4,), (4,), (4,)]
         y_out, grad_w_out, grad_x, grad_w_qkv, grad_b_qkv, sums, grad_w_up, grad_b_up, grad_w_down, _, _ = single_call(
-            functools.partial(backward_kernel, dims), 'backward', 1, ins, (0, 1, 2, 3, 4, 5, 8, 9, 10, 11, 12, 13, 14, 15, 16, 17, 20, 21, 22, 23), outs, (0, 9, 10), scratch)
+            functools.partial(backward_kernel, dims), 'backward', 1, ins, set(range(len(ins))) - {6, 7, 18, 19}, outs, (0, 9, 10), scratch)
         moved = (y_out, grad_x, grad_w_qkv, grad_w_out, grad_w_up, grad_w_down)
         ins = moved + (sums, grad_b_up, grad_b_qkv)
         vector = shape((width,), F32)

time: 209 us -> 191 us (0.914)
  Pallas kernels: 208 us -> 190 us
    pallas_call x3, Pallas kernels: 208 us -> 190 us  [single_call(): pl.pallas_call(kernel, out_shape=outs, in_specs=[ANY_SPEC if i in in_any...]
where the time goes in v4:
time: 191 us
  Pallas kernels  190 us (99%)
    pallas_call x3, Pallas kernels, single_call(): pl.pallas_call(kernel, out_shape=outs, in_specs=[ANY_SPEC if i in in_any...  190 us

profile of v4, /device:TPU:0, one launch (start us, length us, event | category | flops | bytes accessed | tf_op | source)
XLA Modules:
  0.0 191.0 jit_solution(660350268142868868)
XLA Ops:
  0.6 87.1 %forward.1 = (bf16[1024,640]{1,0:T(8,128)(2,1)}, bf16[4,2,240,640]{3,2,1,0:T(8,128)(2,1)}, bf16[1024,640]{1,0:T(8,128)(2,1)}, bf16[20,48,1024]{2,1,0:T(8,128)(2,...) custom-call(bf16[4,256,640]{2,1,0:T(8,128)(2,1)} %x_ref.1, ...), custom_call_target="tpu_custom_call" | custom-call | tf_op jit(solution)/shard_map/forward/pallas_call | solution.py:602
  87.7 95.7 %backward.1 = (bf16[4,256,640]{2,1,0:T(8,128)(2,1)}, f32[160,640]{1,0:T(8,128)}, bf16[4,256,640]{2,1,0:T(8,128)(2,1)}, f32[480,640]{1,0:T(8,128)}, f32[8,480]{1,...) custom-call(bf16[20,48,1024]{2,1,0:T(8,128)(2,1)} %get-tuple-element, ...), custom_call_target="tpu_custom_call" | custom-call | tf_op jit(solution)/shard_map/backward/pallas_call | solution.py:602
  183.4 7.4 %finish.1 = (bf16[4,256,640]{2,1,0:T(8,128)(2,1)}, bf16[4,256,640]{2,1,0:T(8,128)(2,1)}, f32[480,640]{1,0:T(8,128)}, f32[160,640]{1,0:T(8,128)}, f32[640,640]{1,...) custom-call(bf16[4,256,640]{2,1,0:T(8,128)(2,1)} %get-tuple-element., ...), custom_call_target="tpu_custom_call" | custom-call | tf_op jit(solution)/shard_map/finish/pallas_call | solution.py:602

commit v5 on v4

--- a/solution.py
+++ b/solution.py
@@ -568,8 +568,14 @@
     moved, small = refs[:6], refs[6:9]
     outs, vectors, bias_up, bias_qkv = refs[9:15], refs[15:21], refs[21], refs[22]
     bufs, load_sem, store_sem = refs[23:29], refs[29], refs[30]
-    loads = [pltpu.make_async_copy(source, buf, load_sem.at[i]) for i, (source, buf) in enumerate(zip(moved, bufs))]
-    stores = [pltpu.make_async_copy(buf, dst, store_sem.at[i]) for i, (buf, dst) in enumerate(zip(bufs, outs))]
+    loads, stores = [], []
+    for source, buf, dst in zip(moved, bufs, outs):
+        rows, *_ = source.shape
+        half = rows // 2
+        for at in (slice(half), slice(half, rows)):
+            sem = len(loads)
+            loads.append(pltpu.make_async_copy(source.at[at], buf.at[at], load_sem.at[sem]))
+            stores.append(pltpu.make_async_copy(buf.at[at], dst.at[at], store_sem.at[sem]))
     for load in loads:
         load.start()
     for load, store in zip(loads, stores):
@@ -665,7 +671,7 @@
         moved_shapes = [shape(a.shape, a.dtype) for a in moved]
         outs = moved_shapes + [vector] * 6 + [shape((ff,), F32), shape((local_heads, 3, head_dim), F32)]
         y_out, grad_x, grad_w_qkv, grad_w_out, grad_w_up, grad_w_down, *vectors, grad_b_up, grad_b_qkv = single_call(
-            finish_kernel, 'finish', None, ins, range(6), outs, range(6), moved_shapes + [(6,), (6,)])
+            finish_kernel, 'finish', None, ins, range(6), outs, range(6), moved_shapes + [(12,), (12,)])
         grad_w_qkv = grad_w_qkv.reshape(3, local_heads, head_dim, width).transpose(0, 3, 1, 2)
         grad_b_qkv = grad_b_qkv.transpose(1, 0, 2)
         grad_w_out = grad_w_out.reshape(local_heads, head_dim, width)

time: 191 us -> 191 us (level)
  no operation moved by 1% of the time
where the time goes in v5:
time: 191 us
  Pallas kernels  190 us (99%)
    pallas_call x3, Pallas kernels, single_call(): pl.pallas_call(kernel, out_shape=outs, in_specs=[ANY_SPEC if i in in_any...  190 us

profile of v5, /device:TPU:0, one launch (start us, length us, event | category | flops | bytes accessed | tf_op | source)
XLA Modules:
  0.0 191.1 jit_solution(340639736503818140)
XLA Ops:
  0.6 87.1 %forward.1 = (bf16[1024,640]{1,0:T(8,128)(2,1)}, bf16[4,2,240,640]{3,2,1,0:T(8,128)(2,1)}, bf16[1024,640]{1,0:T(8,128)(2,1)}, bf16[20,48,1024]{2,1,0:T(8,128)(2,...) custom-call(bf16[4,256,640]{2,1,0:T(8,128)(2,1)} %x_ref.1, ...), custom_call_target="tpu_custom_call" | custom-call | tf_op jit(solution)/shard_map/forward/pallas_call | solution.py:608
  87.7 95.7 %backward.1 = (bf16[4,256,640]{2,1,0:T(8,128)(2,1)}, f32[160,640]{1,0:T(8,128)}, bf16[4,256,640]{2,1,0:T(8,128)(2,1)}, f32[480,640]{1,0:T(8,128)}, f32[8,480]{1,...) custom-call(bf16[20,48,1024]{2,1,0:T(8,128)(2,1)} %get-tuple-element, ...), custom_call_target="tpu_custom_call" | custom-call | tf_op jit(solution)/shard_map/backward/pallas_call | solution.py:608
  183.4 7.5 %finish.1 = (bf16[4,256,640]{2,1,0:T(8,128)(2,1)}, bf16[4,256,640]{2,1,0:T(8,128)(2,1)}, f32[480,640]{1,0:T(8,128)}, f32[160,640]{1,0:T(8,128)}, f32[640,640]{1,...) custom-call(bf16[4,256,640]{2,1,0:T(8,128)(2,1)} %get-tuple-element., ...), custom_call_target="tpu_custom_call" | custom-call | tf_op jit(solution)/shard_map/finish/pallas_call | solution.py:608
